TPU v7x, 256 devices: a whole 4x4x8 slice. The times are simulated.
256 devices in a mesh: pa: 16 (over x_hi, z), gz: 16 (over x_lo, y, core).
Axes of the slice: x: 4 (x_hi: 2, x_lo: 2; x = x_hi * 2 + x_lo), y: 4, z: 8, core: 2. Of those that a mesh axis runs over, the one named last changes fastest.
Arguments:
- source: float32 [128, 768, 768], P('gz', 'pa'), may hold values from -24 to 24
- cell_width: float32 [128], P('gz'), may hold values from 0.5 to 2
Outputs:
- potential: float32 [128, 768, 768], P('gz', 'pa')
All inputs are finite; a program needn't handle non-finite values.
Results may differ from a plain program's by a relative error of at most 0.00085.
Values sent between devices are 32-bit elements; how exact they have to be, the bound alone decides.
No kernel may reach another device: no remote copies, remote signals or barrier semaphores. Data moves between devices by JAX's collectives and lax.ppermute only.
A program may use at most 64 MiB of HBM per device.

v0:
```python
import functools
import math

import numpy as np

import jax
import jax.numpy as jnp
from jax import lax
from jax.experimental import pallas as pl
from jax.experimental.pallas import tpu as pltpu
from jax.sharding import PartitionSpec as P

ALL = ("pa", "gz")
LANES = 128
SUB = 8
VMEM = pltpu.MemorySpace.VMEM


def halves(table):
    table = table.astype(np.float32)
    high = table.astype(jnp.bfloat16)
    low = (table - high.astype(np.float32)).astype(jnp.bfloat16)
    return jnp.asarray(high), jnp.asarray(low)


def cosine_rows(width):
    k = np.arange(width)
    phases = k[:, None] * (2 * k[None, :] + 1) % (4 * width)
    weights = np.where(k == 0, math.sqrt(1.0 / width), math.sqrt(2.0 / width))
    return weights[:, None] * np.cos(phases * (math.pi / (2 * width)))


def sine_rows(width):
    k = np.arange(1, width + 1)
    phases = k[:, None] * k[None, :] % (2 * (width + 1))
    return math.sqrt(2.0 / (width + 1)) * np.sin(phases * (math.pi / (width + 1)))


def eigen_first(wavenumber, width):
    return 4.0 * jnp.square(jnp.sin(wavenumber.astype(jnp.float32) * (math.pi / (2 * width))))


def eigen_second(width):
    wavenumber = jnp.arange(1, width + 1, dtype=jnp.int32).astype(jnp.float32)
    return 4.0 * jnp.square(jnp.sin(wavenumber * (math.pi / (2 * (width + 1)))))


def split(x):
    high = x.astype(jnp.bfloat16)
    return high, (x - high.astype(jnp.float32)).astype(jnp.bfloat16)


def dot3(a, b, dims):
    dot = functools.partial(
        lax.dot_general, dimension_numbers=(dims, ((), ())), preferred_element_type=jnp.float32
    )
    return dot(a[0], b[0]) + dot(a[1], b[0]) + dot(a[0], b[1])


def swap_groups(blocks, group):
    n = len(blocks)
    lanes = n * group
    lane = lax.broadcasted_iota(jnp.int32, blocks[0].shape, 1)
    blocks = list(blocks)
    d = 1
    while d < n:
        keep = (lane & (d * group)) == 0
        for i in range(n):
            if i & d:
                continue
            a, b = blocks[i], blocks[i + d]
            blocks[i] = jnp.where(keep, a, pltpu.roll(b, d * group, 1))
            blocks[i + d] = jnp.where(keep, pltpu.roll(a, lanes - d * group, 1), b)
        d *= 2
    return blocks


def forward_x(src_ref, wid_ref, ch_ref, cl_ref, out_ref, acc_ref, *, devices, group):
    depth, rows, _ = src_ref.shape
    parts = rows // group
    owned = ch_ref.shape[0] // devices
    stride = owned * parts + 1
    x = jnp.concatenate(
        [src_ref[z, pl.ds(m * group, group), :] for m in range(parts) for z in range(depth)], 0
    )
    acc_ref[...] = dot3((ch_ref[...], cl_ref[...]), split(x), ((1,), (1,)))
    widths = jnp.broadcast_to(wid_ref[...], (SUB, LANES))
    for t in range(devices // SUB):
        for kk in range(owned):
            for m in range(parts):
                out_ref[pl.ds(t * SUB * stride + kk * parts + m, SUB, stride=stride), :] = acc_ref[
                    pl.ds(kk * devices + t * SUB, SUB), pl.ds(m * LANES, LANES)
                ]
        out_ref[pl.ds(t * SUB * stride + owned * parts, SUB, stride=stride), :] = widths


def backward_x(msg_ref, ch_ref, cl_ref, out_ref, z_ref, *, devices, group):
    depth, rows, _ = out_ref.shape
    parts = rows // group
    owned = ch_ref.shape[0] // devices
    stride = owned * parts
    for t in range(devices // SUB):
        for kk in range(owned):
            for m in range(parts):
                z_ref[pl.ds(kk * devices + t * SUB, SUB), pl.ds(m * LANES, LANES)] = msg_ref[
                    pl.ds(t * SUB * stride + kk * parts + m, SUB, stride=stride), :
                ]
    y = dot3(split(z_ref[...].T), (ch_ref[...], cl_ref[...]), ((1,), (0,)))
    for m in range(parts):
        for z in range(depth):
            out_ref[z, pl.ds(m * group, group), :] = y[(m * depth + z) * group :][:group]


def middle(
    msg_ref, sh_ref, sl_ref, ek_ref, el_ref, out_ref, a_ref, wid_ref, left_ref, right_ref, red_ref,
    *, peers, blocks, depth, parts, group, tile
):
    owned = ek_ref.shape[0]
    wide = el_ref.shape[1]
    stride_in, stride_out = owned * parts + 1, owned * parts
    halfs = peers // depth
    rows = depth * blocks
    cells = wide // LANES
    pitch = -(-owned * cells // SUB) * SUB

    def where(kk, zi):
        return pl.ds(kk * rows + zi * blocks, blocks)

    wid_ref[...] = jnp.zeros(wid_ref.shape, jnp.float32)
    wid_ref[pl.ds(SUB, blocks), :] = msg_ref[pl.ds(stride_in - 1, blocks, stride=stride_in), :]
    width = wid_ref[pl.ds(SUB, blocks), :]
    before, after = wid_ref[pl.ds(SUB - 1, blocks), :], wid_ref[pl.ds(SUB + 1, blocks), :]
    column = lambda a, i: a[:, i : i + 1]
    width_of = [column(width, i) for i in range(depth)]
    padded = [column(before, depth - 1), *width_of, column(after, 0)]
    link = [2.0 / (padded[i] + padded[i + 1]) for i in range(depth + 1)]
    lower, upper = link[:-1], link[1:]

    for kk in range(owned):
        for m in range(parts):
            for h in range(halfs):
                got = [
                    msg_ref[
                        pl.ds((h * depth + g) * blocks * stride_in + kk * parts + m, blocks, stride=stride_in), :
                    ]
                    for g in range(depth)
                ]
                for zi, block in enumerate(swap_groups(got, group)):
                    a_ref[where(kk, zi), pl.ds((m * halfs + h) * LANES, LANES)] = block
    table = (sh_ref[...], sl_ref[...])
    a_ref[...] = dot3(split(a_ref[...]), table, ((1,), (0,)))

    def scatter(index, kk, t, value):
        for s in range(blocks // SUB):
            for c in range(tile // LANES):
                row = s * SUB * pitch + kk * cells + t * (tile // LANES) + c
                red_ref[index, pl.ds(row, SUB, stride=pitch), :] = value[
                    s * SUB : s * SUB + SUB, c * LANES : c * LANES + LANES
                ]

    for kk in range(owned):
        for t in range(wide // tile):
            cols = pl.ds(t * tile, tile)
            eigen = ek_ref[kk : kk + 1, :] + el_ref[:, cols]
            diagonal = lambda i: (lower[i] + upper[i]) + width_of[i] * eigen
            forcing = lambda i: width_of[i] * a_ref[where(kk, i), cols]
            left, right, value = [None], [None], [None]
            for i in range(1, depth):
                if i == 1:
                    inverse = 1.0 / diagonal(i)
                    left.append(-(inverse * lower[i]))
                    value.append(inverse * forcing(i))
                else:
                    inverse = 1.0 / (diagonal(i) + lower[i] * right[-1])
                    below = inverse * lower[i]
                    left.append(below * left[-1])
                    value.append(inverse * forcing(i) + below * value[-1])
                right.append(-(inverse * upper[i]))
                if i < depth - 1:
                    left_ref[where(kk, i), cols] = left[i]
                    right_ref[where(kk, i), cols] = right[i]
                    a_ref[where(kk, i), cols] = value[i]
            inner_left, inner_right, inner = left[depth - 2], right[depth - 2], value[depth - 2]
            for i in range(depth - 3, 0, -1):
                inner_left = left[i] - right[i] * inner_left
                inner_right = -(right[i] * inner_right)
                inner = value[i] - right[i] * inner
            inverse = 1.0 / (diagonal(0) + upper[0] * inner_left)
            scatter(0, kk, t, -(inverse * lower[0]))
            scatter(1, kk, t, inverse * upper[0] * inner_right)
            scatter(2, kk, t, inverse * (forcing(0) + upper[0] * inner))
            scatter(3, kk, t, left[depth - 1])
            scatter(4, kk, t, right[depth - 1])
            scatter(5, kk, t, value[depth - 1])

    ratio = rhs = None
    for q in range(blocks):
        at = pl.ds(q * pitch, pitch)
        head_below, head_above, head_in, tail_below, tail_above, tail_in = (
            red_ref[i, at, :] for i in range(6)
        )
        if q == 0:
            head_ratio, head_rhs = head_above, head_in
        else:
            divided = 1.0 / (1.0 - head_below * ratio)
            head_ratio = head_above * divided
            head_rhs = (head_in - head_below * rhs) * divided
        divided = 1.0 / (1.0 - tail_below * head_ratio)
        ratio = tail_above * divided
        rhs = (tail_in - tail_below * head_rhs) * divided
        for i, value in ((1, head_ratio), (2, head_rhs), (4, ratio), (5, rhs)):
            red_ref[i, at, :] = value
    following = None
    for q in range(blocks - 1, -1, -1):
        at = pl.ds(q * pitch, pitch)
        tail = red_ref[5, at, :]
        if following is not None:
            tail = tail - red_ref[4, at, :] * following
        following = red_ref[2, at, :] - red_ref[1, at, :] * tail
        red_ref[0, at, :] = following
        red_ref[3, at, :] = tail

    for kk in range(owned):
        for s in range(blocks // SUB):
            for c in range(cells):
                row = s * SUB * pitch + kk * cells + c
                cols = pl.ds(c * LANES, LANES)
                for zi, index in ((0, 0), (depth - 1, 3)):
                    a_ref[pl.ds(kk * rows + zi * blocks + s * SUB, SUB), cols] = red_ref[
                        index, pl.ds(row, SUB, stride=pitch), :
                    ]
        for t in range(wide // tile):
            cols = pl.ds(t * tile, tile)
            head, following = a_ref[where(kk, 0), cols], a_ref[where(kk, depth - 1), cols]
            for i in range(depth - 2, 0, -1):
                at = where(kk, i)
                following = (a_ref[at, cols] - left_ref[at, cols] * head) - right_ref[at, cols] * following
                a_ref[at, cols] = following

    a_ref[...] = dot3(split(a_ref[...]), table, ((1,), (1,)))
    for kk in range(owned):
        for m in range(parts):
            for h in range(halfs):
                lanes = pl.ds((m * halfs + h) * LANES, LANES)
                sent = swap_groups([a_ref[where(kk, zi), lanes] for zi in range(depth)], group)
                for g, block in enumerate(sent):
                    row = (h * depth + g) * blocks * stride_out + kk * parts + m
                    out_ref[pl.ds(row, blocks, stride=stride_out), :] = block


def call(kernel, name, out, args, scratch):
    return pl.pallas_call(
        kernel,
        name=name,
        out_shape=jax.ShapeDtypeStruct(out, jnp.float32),
        in_specs=[pl.BlockSpec(memory_space=VMEM)] * len(args),
        out_specs=pl.BlockSpec(memory_space=VMEM),
        scratch_shapes=[pltpu.VMEM(s, jnp.float32) for s in scratch],
    )(*args)


def exchange(rows, devices):
    flat = rows.reshape(devices, 1, -1)
    return lax.all_to_all(flat, ALL, split_axis=0, concat_axis=0, tiled=True).reshape(-1, LANES)


def on_device(source, cell_width):
    depth, rows, width_x = source.shape
    peers, blocks = lax.axis_size("pa"), lax.axis_size("gz")
    devices = peers * blocks
    width_y = rows * peers
    owned = width_x // devices
    group = LANES // depth
    parts = rows // group

    cosines = halves(cosine_rows(width_x))
    order = np.arange(width_y).reshape(peers, parts, group).transpose(1, 0, 2).reshape(-1)
    sines = halves(sine_rows(width_y)[order])
    widths = jnp.pad(cell_width, (0, LANES - depth))[None]
    sent = call(
        functools.partial(forward_x, devices=devices, group=group), "forward_x",
        (devices * (owned * parts + 1), LANES), (source, widths, *cosines),
        [(width_x, depth * rows)],
    )
    own_k = jnp.arange(owned, dtype=jnp.int32) * devices + lax.axis_index(ALL)
    eigen_x, eigen_y = eigen_first(own_k, width_x)[:, None], eigen_second(width_y)[None]
    cells = width_y // LANES
    pitch = -(-owned * cells // SUB) * SUB
    size = (owned * depth * blocks, width_y)
    back = call(
        functools.partial(
            middle, peers=peers, blocks=blocks, depth=depth, parts=parts, group=group, tile=TILE
        ),
        "middle", (devices * owned * parts, LANES),
        (exchange(sent, devices), *sines, eigen_x, eigen_y),
        [size, (blocks + 2 * SUB, LANES), size, size, (6, blocks * pitch, LANES)],
    )
    return call(
        functools.partial(backward_x, devices=devices, group=group), "backward_x", source.shape,
        (exchange(back, devices), *cosines), [(width_x, depth * rows)],
    )


TILE = 384


def solution(mesh):
    return jax.shard_map(
        on_device,
        mesh=mesh,
        in_specs=(P("gz", "pa", None), P("gz")),
        out_specs=P("gz", "pa", None),
        check_vma=False,
    )
```

profile of v0, /device:TPU:1, one launch (start us, length us, event | category | flops | bytes accessed | tf_op | source)
XLA Modules:
  0.0 114.0 jit_solution(8615399653476351245)
XLA Ops:
  0.0 1.2 %pad_bitcast_fusion.wid_ref = f32[1,128]{1,0:T(1,128)} fusion(f32[8]{0:T(128)} %param.7), kind=kLoop, calls=%fused_computation.2 | loop fusion | bytes 544 | tf_op jit(solution)/shard_map/broadcast_in_dim | solution.py:279
  1.2 5.1 %forward_x.1 = f32[2560,128]{1,0:T(8,128)} custom-call(f32[8,48,768]{2,1,0:T(8,128)} %src_ref.1, f32[1,128]{1,0:T(1,128)} %pad_bitcast_fusion.wid_ref, bf16[768,768]{1,0:T(8,128)(2,1)} %constant.31.clone.ch_ref, bf16[768,768]{1,0:T(8,128)(2,1)} %constant.32.clone.cl_ref), custom_call_target="tpu_custom_call" | custom-call | tf_op jit(solution)/shard_map/forward_x/pallas_call | solution.py:252
  6.2 15.6 %all-to-all-start = ((f32[256,1,1280]{2,1,0:T(1,128)}), f32[256,1,1280]{2,1,0:T(1,128)S(1)}, u32[]{:S(2)}, u32[]{:S(2)}) async-start(f32[256,1,1280]{2,1,0:T(1,128)} %bitcast.6), calls=%async_computation | async-start | bytes 2621440 | tf_op jit(solution)/shard_map/all_to_all | solution.py:264
  21.9 0.6 multiply_multiply_fusion.1.ek_ref
  22.5 0.7 multiply_multiply_fusion.el_ref
  23.2 34.1 %all-to-all-done = f32[256,1,1280]{2,1,0:T(1,128)S(1)} async-done(((f32[256,1,1280]{2,1,0:T(1,128)}), f32[256,1,1280]{2,1,0:T(1,128)S(1)}, u32[]{:S(2)}, u32[]{:S(2)}) %all-to-all-start) | async-done | bytes 1310752 | tf_op jit(solution)/shard_map/all_to_all | solution.py:264
  57.3 0.0 copy-start
  57.3 1.1 copy-done
  58.4 10.1 %middle.1 = f32[2304,128]{1,0:T(8,128)} custom-call(f32[2560,128]{1,0:T(8,128)} %bitcast.7, bf16[768,768]{1,0:T(8,128)(2,1)} %constant.33.clone.sh_ref, bf16[768,768]{1,0:T(8,128)(2,1)} %constant.34.clone.sl_ref, f32[3,1]{1,0:T(4,128)} %multiply_multiply_fusion.1.ek_ref, f32[1,768]{1,0:T(1,128)} %multiply_multiply_fusion.el_ref), custom_call_target="tpu_custom_call" | custom-call | tf_op jit(solution)/shard_map/middle/pallas_call | solution.py:252
  68.4 40.9 %all_to_all.10 = f32[256,1,1152]{2,1,0:T(1,128)} all-to-all(f32[256,1,1152]{2,1,0:T(1,128)} %bitcast.8), channel_id=1, replica_groups=mesh['pa'=16,'gz'=16] {'pa','gz'}, dimensions={0} | all-to-all | bytes 2359296 | tf_op jit(solution)/shard_map/all_to_all | solution.py:264
  109.3 4.7 %backward_x.1 = f32[8,48,768]{2,1,0:T(8,128)} custom-call(f32[2304,128]{1,0:T(8,128)} %bitcast.9, bf16[768,768]{1,0:T(8,128)(2,1)} %constant.31.clone.ch_ref, bf16[768,768]{1,0:T(8,128)(2,1)} %constant.32.clone.cl_ref), custom_call_target="tpu_custom_call" | custom-call | tf_op jit(solution)/shard_map/backward_x/pallas_call | solution.py:252
Async XLA Ops:
  6.2 51.1 %all-to-all-start = ((f32[256,1,1280]{2,1,0:T(1,128)}), f32[256,1,1280]{2,1,0:T(1,128)S(1)}, u32[]{:S(2)}, u32[]{:S(2)}) async-start(f32[256,1,1280]{2,1,0:T(1,128)} %bitcast.6), calls=%async_computation | async-start | bytes 2621440 | tf_op jit(solution)/shard_map/all_to_all | solution.py:264
  57.3 1.1 copy-start
where the time goes:
time: 114 us
  blocking collectives  40.9 us (36%)
  waiting for transfers between devices  34.1 us (30%)
  Pallas kernels  19.8 us (17%)
  starting transfers between devices  15.6 us (14%)
  local copies, waits for them, and re-layouts  2.23 us (2%)
  other arithmetic  1.33 us (1%)
    all_to_all x1, blocking collectives, exchange(): lax.all_to_all(flat, ALL, split_axis=0, concat_axis=0, tiled=True)  40.9 us
    all_to_all x1, waiting for transfers between devices, exchange(): lax.all_to_all(flat, ALL, split_axis=0, concat_axis=0, tiled=True)  34.1 us
    pallas_call x3, Pallas kernels, call(): pl.pallas_call(kernel, name=name, out_shape=jax.ShapeDtypeStruct(out, jnp...  19.8 us
    all_to_all x1, starting transfers between devices, exchange(): lax.all_to_all(flat, ALL, split_axis=0, concat_axis=0, tiled=True)  15.6 us
  transfers between devices with their start and end apart: 1, of which 1 were waited for; matrix products, arithmetic and copies ran while one was open for 1% of the time, Pallas kernels for 0%

commit v1 on v0

v1 whole, which is shorter than its diff:
```python
import functools
import math

import numpy as np

import jax
import jax.numpy as jnp
from jax import lax
from jax.experimental import pallas as pl
from jax.experimental.pallas import tpu as pltpu
from jax.sharding import PartitionSpec as P

ALL = ("pa", "gz")
LANES = 128
SUB = 8
VMEM = pltpu.MemorySpace.VMEM


def halves(table):
    table = table.astype(np.float32)
    high = table.astype(jnp.bfloat16)
    low = (table - high.astype(np.float32)).astype(jnp.bfloat16)
    return jnp.asarray(high), jnp.asarray(low)


def cosine_rows(width):
    k = np.arange(width)
    phases = k[:, None] * (2 * k[None, :] + 1) % (4 * width)
    weights = np.where(k == 0, math.sqrt(1.0 / width), math.sqrt(2.0 / width))
    return weights[:, None] * np.cos(phases * (math.pi / (2 * width)))


def sine_rows(width):
    k = np.arange(1, width + 1)
    phases = k[:, None] * k[None, :] % (2 * (width + 1))
    return math.sqrt(2.0 / (width + 1)) * np.sin(phases * (math.pi / (width + 1)))


def eigen_first(wavenumber, width):
    return 4.0 * jnp.square(jnp.sin(wavenumber.astype(jnp.float32) * (math.pi / (2 * width))))


def eigen_second(width):
    wavenumber = jnp.arange(1, width + 1, dtype=jnp.int32).astype(jnp.float32)
    return 4.0 * jnp.square(jnp.sin(wavenumber * (math.pi / (2 * (width + 1)))))


def split(x):
    high = x.astype(jnp.bfloat16)
    return high, (x - high.astype(jnp.float32)).astype(jnp.bfloat16)


def dot3(a, b, dims):
    lhs = jnp.concatenate([a[0], a[1], a[0]], dims[0][0])
    rhs = jnp.concatenate([b[0], b[0], b[1]], dims[1][0])
    return lax.dot_general(lhs, rhs, (dims, ((), ())), preferred_element_type=jnp.float32)


def swap_groups(blocks, group):
    n = len(blocks)
    lanes = n * group
    lane = lax.broadcasted_iota(jnp.int32, blocks[0].shape, 1)
    blocks = list(blocks)
    d = 1
    while d < n:
        keep = (lane & (d * group)) == 0
        for i in range(n):
            if i & d:
                continue
            a, b = blocks[i], blocks[i + d]
            blocks[i] = jnp.where(keep, a, pltpu.roll(b, d * group, 1))
            blocks[i + d] = jnp.where(keep, pltpu.roll(a, lanes - d * group, 1), b)
        d *= 2
    return blocks


def forward_x(src_ref, ch_ref, cl_ref, out_ref, xh_ref, xl_ref, acc_ref, *, group):
    depth, rows, width = src_ref.shape
    parts = rows // group
    owned, some, _ = ch_ref.shape
    stride = owned * parts

    @pl.when(pl.program_id(0) == 0)
    def _():
        for m in range(parts):
            for z in range(depth):
                at = pl.ds((m * depth + z) * group, group)
                xh_ref[at, :], xl_ref[at, :] = split(src_ref[z, pl.ds(m * group, group), :])

    table = (ch_ref[...].reshape(owned * some, width), cl_ref[...].reshape(owned * some, width))
    acc_ref[...] = dot3(table, (xh_ref[...], xl_ref[...]), ((1,), (1,)))
    for t in range(some // SUB):
        for kk in range(owned):
            for m in range(parts):
                out_ref[pl.ds(t * SUB * stride + kk * parts + m, SUB, stride=stride), :] = acc_ref[
                    pl.ds(kk * some + t * SUB, SUB), pl.ds(m * LANES, LANES)
                ]


def backward_x(msg_ref, ch_ref, cl_ref, out_ref, z_ref, zh_ref, zl_ref, *, group):
    depth, rows, _ = out_ref.shape
    parts = rows // group
    owned, devices, some = ch_ref.shape
    stride = owned * parts
    table = [ref[...].reshape(owned * devices, some) for ref in (ch_ref, cl_ref)]

    @pl.when(pl.program_id(0) == 0)
    def _():
        for t in range(devices // SUB):
            for kk in range(owned):
                for m in range(parts):
                    z_ref[pl.ds(kk * devices + t * SUB, SUB), pl.ds(m * LANES, LANES)] = msg_ref[
                        pl.ds(t * SUB * stride + kk * parts + m, SUB, stride=stride), :
                    ]
        zh_ref[...], zl_ref[...] = split(z_ref[...].T)

    y = dot3((zh_ref[...], zl_ref[...]), table, ((1,), (0,)))
    for m in range(parts):
        for z in range(depth):
            out_ref[z, pl.ds(m * group, group), :] = y[(m * depth + z) * group :][:group]


def coefficients(wid_in_ref, ek_ref, el_ref, cell_ref, block_ref, wid_ref, red_ref, *, depth, tile):
    blocks = wid_in_ref.shape[0]
    owned, wide = ek_ref.shape[0], el_ref.shape[1]
    rows = depth * blocks
    cells = wide // LANES
    pitch = -(-owned * cells // SUB) * SUB

    wid_ref[...] = jnp.zeros(wid_ref.shape, jnp.float32)
    wid_ref[pl.ds(SUB, blocks), :] = wid_in_ref[...]
    width = wid_ref[pl.ds(SUB, blocks), :]
    before, after = wid_ref[pl.ds(SUB - 1, blocks), :], wid_ref[pl.ds(SUB + 1, blocks), :]
    column = lambda a, i: a[:, i : i + 1]
    width_of = [column(width, i) for i in range(depth)]
    padded = [column(before, depth - 1), *width_of, column(after, 0)]
    link = [2.0 / (padded[i] + padded[i + 1]) for i in range(depth + 1)]
    lower, upper = link[:-1], link[1:]
    red_ref[...] = jnp.zeros(red_ref.shape, jnp.float32)

    def scatter(index, kk, t, value):
        for s in range(blocks // SUB):
            for c in range(tile // LANES):
                row = s * SUB * pitch + kk * cells + t * (tile // LANES) + c
                red_ref[index, pl.ds(row, SUB, stride=pitch), :] = value[
                    s * SUB : s * SUB + SUB, c * LANES : c * LANES + LANES
                ]

    for kk in range(owned):
        for t in range(wide // tile):
            cols = pl.ds(t * tile, tile)
            eigen = ek_ref[kk : kk + 1, :] + el_ref[:, cols]
            diagonal = lambda i: (lower[i] + upper[i]) + width_of[i] * eigen
            left, right = [None], [None]
            for i in range(1, depth):
                if i == 1:
                    inverse = 1.0 / diagonal(i)
                    below = jnp.zeros(inverse.shape, jnp.float32)
                    left.append(-(inverse * lower[i]))
                else:
                    inverse = 1.0 / (diagonal(i) + lower[i] * right[-1])
                    below = inverse * lower[i]
                    left.append(below * left[-1])
                right.append(-(inverse * upper[i]))
                at = pl.ds(kk * rows + i * blocks, blocks)
                for index, value in enumerate((inverse * width_of[i], below, left[i], right[i])):
                    cell_ref[index, at, cols] = value
            inner_left, inner_right = left[depth - 2], right[depth - 2]
            for i in range(depth - 3, 0, -1):
                inner_left = left[i] - right[i] * inner_left
                inner_right = -(right[i] * inner_right)
            inverse = 1.0 / (diagonal(0) + upper[0] * inner_left)
            at = pl.ds(kk * rows, blocks)
            above = inverse * upper[0]
            zero = jnp.zeros(inverse.shape, jnp.float32)
            for index, value in enumerate((inverse * width_of[0], above, zero, zero)):
                cell_ref[index, at, cols] = value
            scatter(0, kk, t, -(inverse * lower[0]))
            scatter(1, kk, t, above * inner_right)
            scatter(2, kk, t, left[depth - 1])
            scatter(3, kk, t, right[depth - 1])

    ratio = None
    for q in range(blocks):
        at = pl.ds(q * pitch, pitch)
        head_below, head_above, tail_below, tail_above = (red_ref[i, at, :] for i in range(4))
        if q == 0:
            head_own = jnp.ones(head_above.shape, jnp.float32)
            head_up = jnp.zeros(head_above.shape, jnp.float32)
            head_ratio = head_above
        else:
            head_own = 1.0 / (1.0 - head_below * ratio)
            head_up = -(head_below * head_own)
            head_ratio = head_above * head_own
        tail_own = 1.0 / (1.0 - tail_below * head_ratio)
        ratio = tail_above * tail_own
        found = (head_own, head_up, tail_own, -(tail_below * tail_own), head_ratio, ratio)
        for index, value in enumerate(found):
            block_ref[index, at, :] = value


def middle(
    msg_ref, sh_in, sl_in, cell_in, block_in, out_ref, a_ref, red_ref, sh_ref, sl_ref, cell_ref, block_ref, sems,
    *, peers, blocks, depth, parts, group, owned, tile
):
    copies = [
        pltpu.make_async_copy(source, target, sems.at[i])
        for i, (source, target) in enumerate(
            ((sh_in, sh_ref), (sl_in, sl_ref), (cell_in, cell_ref), (block_in, block_ref))
        )
    ]
    for copy in copies:
        copy.start()
    wide = sh_in.shape[1]
    stride = owned * parts
    halfs = peers // depth
    rows = depth * blocks
    cells = wide // LANES
    pitch = -(-owned * cells // SUB) * SUB

    def where(kk, zi):
        return pl.ds(kk * rows + zi * blocks, blocks)

    for kk in range(owned):
        for m in range(parts):
            for h in range(halfs):
                got = [
                    msg_ref[pl.ds((h * depth + g) * blocks * stride + kk * parts + m, blocks, stride=stride), :]
                    for g in range(depth)
                ]
                for zi, block in enumerate(swap_groups(got, group)):
                    a_ref[where(kk, zi), pl.ds((m * halfs + h) * LANES, LANES)] = block
    copies[0].wait()
    copies[1].wait()
    table = (sh_ref[...], sl_ref[...])
    for kk in range(owned):
        at = pl.ds(kk * rows, rows)
        a_ref[at, :] = dot3(split(a_ref[at, :]), table, ((1,), (0,)))
    copies[2].wait()
    copies[3].wait()

    def scatter(index, kk, t, value):
        for s in range(blocks // SUB):
            for c in range(tile // LANES):
                row = s * SUB * pitch + kk * cells + t * (tile // LANES) + c
                red_ref[index, pl.ds(row, SUB, stride=pitch), :] = value[
                    s * SUB : s * SUB + SUB, c * LANES : c * LANES + LANES
                ]

    red_ref[...] = jnp.zeros(red_ref.shape, jnp.float32)
    for kk in range(owned):
        for t in range(wide // tile):
            cols = pl.ds(t * tile, tile)
            value = [None]
            for i in range(1, depth):
                at = where(kk, i)
                now = cell_ref[0, at, cols] * a_ref[at, cols]
                if i > 1:
                    now = now + cell_ref[1, at, cols] * value[-1]
                value.append(now)
                if i < depth - 1:
                    a_ref[at, cols] = now
            inner = value[depth - 2]
            for i in range(depth - 3, 0, -1):
                inner = value[i] - cell_ref[3, where(kk, i), cols] * inner
            at = where(kk, 0)
            scatter(0, kk, t, cell_ref[0, at, cols] * a_ref[at, cols] + cell_ref[1, at, cols] * inner)
            scatter(1, kk, t, value[depth - 1])

    rhs = None
    for q in range(blocks):
        at = pl.ds(q * pitch, pitch)
        head = block_ref[0, at, :] * red_ref[0, at, :]
        if rhs is not None:
            head = head + block_ref[1, at, :] * rhs
        rhs = block_ref[2, at, :] * red_ref[1, at, :] + block_ref[3, at, :] * head
        red_ref[0, at, :] = head
        red_ref[1, at, :] = rhs
    following = None
    for q in range(blocks - 1, -1, -1):
        at = pl.ds(q * pitch, pitch)
        tail = red_ref[1, at, :]
        if following is not None:
            tail = tail - block_ref[5, at, :] * following
            red_ref[1, at, :] = tail
        following = red_ref[0, at, :] - block_ref[4, at, :] * tail
        red_ref[0, at, :] = following

    for kk in range(owned):
        for s in range(blocks // SUB):
            for c in range(cells):
                row = s * SUB * pitch + kk * cells + c
                cols = pl.ds(c * LANES, LANES)
                for zi, index in ((0, 0), (depth - 1, 1)):
                    a_ref[pl.ds(kk * rows + zi * blocks + s * SUB, SUB), cols] = red_ref[
                        index, pl.ds(row, SUB, stride=pitch), :
                    ]
        for t in range(wide // tile):
            cols = pl.ds(t * tile, tile)
            head, following = a_ref[where(kk, 0), cols], a_ref[where(kk, depth - 1), cols]
            for i in range(depth - 2, 0, -1):
                at = where(kk, i)
                free = a_ref[at, cols] - cell_ref[2, at, cols] * head
                following = free - cell_ref[3, at, cols] * following
                a_ref[at, cols] = following
        at = pl.ds(kk * rows, rows)
        a_ref[at, :] = dot3(split(a_ref[at, :]), table, ((1,), (1,)))
        for m in range(parts):
            for h in range(halfs):
                lanes = pl.ds((m * halfs + h) * LANES, LANES)
                sent = swap_groups([a_ref[where(kk, zi), lanes] for zi in range(depth)], group)
                for g, block in enumerate(sent):
                    row = (h * depth + g) * blocks * stride + kk * parts + m
                    out_ref[pl.ds(row, blocks, stride=stride), :] = block


WHOLE = pl.BlockSpec(memory_space=VMEM)
STEPS = 2


def call_forward(source, high, low, group):
    depth, rows, width = source.shape
    owned, devices, _ = high.shape
    some = devices // STEPS
    table = pl.BlockSpec((owned, some, width), lambda j: (0, j, 0))
    out = width * depth * rows // LANES
    return pl.pallas_call(
        functools.partial(forward_x, group=group),
        name="forward_x",
        grid=(STEPS,),
        out_shape=jax.ShapeDtypeStruct((out, LANES), jnp.float32),
        in_specs=[pl.BlockSpec(source.shape, lambda j: (0, 0, 0)), table, table],
        out_specs=pl.BlockSpec((out // STEPS, LANES), lambda j: (j, 0)),
        scratch_shapes=[
            pltpu.VMEM((depth * rows, width), jnp.bfloat16),
            pltpu.VMEM((depth * rows, width), jnp.bfloat16),
            pltpu.VMEM((owned * some, depth * rows), jnp.float32),
        ],
    )(source, high, low)


def call_backward(message, high, low, shape, group):
    depth, rows, width = shape
    steps = width // 256
    table = pl.BlockSpec((*high.shape[:2], width // steps), lambda j: (0, 0, j))
    return pl.pallas_call(
        functools.partial(backward_x, group=group),
        name="backward_x",
        grid=(steps,),
        out_shape=jax.ShapeDtypeStruct(shape, jnp.float32),
        in_specs=[pl.BlockSpec(message.shape, lambda j: (0, 0)), table, table],
        out_specs=pl.BlockSpec((depth, rows, width // steps), lambda j: (0, 0, j)),
        scratch_shapes=[
            pltpu.VMEM((width, depth * rows), jnp.float32),
            pltpu.VMEM((depth * rows, width), jnp.bfloat16),
            pltpu.VMEM((depth * rows, width), jnp.bfloat16),
        ],
    )(message, high, low)


def call_coefficients(widths, eigen_x, eigen_y, depth):
    blocks, owned, wide = widths.shape[0], eigen_x.shape[0], eigen_y.shape[1]
    pitch = -(-owned * (wide // LANES) // SUB) * SUB
    shapes = ((4, owned * depth * blocks, wide), (6, blocks * pitch, LANES))
    return pl.pallas_call(
        functools.partial(coefficients, depth=depth, tile=wide // 2),
        name="coefficients",
        out_shape=[jax.ShapeDtypeStruct(s, jnp.float32) for s in shapes],
        in_specs=[WHOLE] * 3,
        out_specs=[WHOLE] * 2,
        scratch_shapes=[
            pltpu.VMEM((blocks + 2 * SUB, LANES), jnp.float32),
            pltpu.VMEM((4, blocks * pitch, LANES), jnp.float32),
        ],
    )(widths, eigen_x, eigen_y)


def call_middle(message, high, low, cell, block, *, peers, blocks, depth, parts, group, owned):
    wide = high.shape[1]
    anywhere = pl.BlockSpec(memory_space=pl.ANY)
    return pl.pallas_call(
        functools.partial(
            middle, peers=peers, blocks=blocks, depth=depth, parts=parts, group=group, owned=owned, tile=wide // 2
        ),
        name="middle",
        out_shape=jax.ShapeDtypeStruct(message.shape, jnp.float32),
        in_specs=[WHOLE, *[anywhere] * 4],
        out_specs=WHOLE,
        scratch_shapes=[
            pltpu.VMEM((owned * depth * blocks, wide), jnp.float32),
            pltpu.VMEM((2, *block.shape[1:]), jnp.float32),
            pltpu.VMEM(high.shape, jnp.bfloat16),
            pltpu.VMEM(low.shape, jnp.bfloat16),
            pltpu.VMEM(cell.shape, jnp.float32),
            pltpu.VMEM(block.shape, jnp.float32),
            pltpu.SemaphoreType.DMA((4,)),
        ],
    )(message, high, low, cell, block)


def exchange(rows, devices):
    flat = rows.reshape(devices, 1, -1)
    return lax.all_to_all(flat, ALL, split_axis=0, concat_axis=0, tiled=True).reshape(-1, LANES)


def all_widths(cell_width, blocks):
    depth = cell_width.shape[0]
    row = lax.broadcasted_iota(jnp.int32, (blocks, LANES), 0)
    held = jnp.where(row == lax.axis_index("gz"), jnp.pad(cell_width, (0, LANES - depth))[None], 0.0)
    step = 1
    while step < blocks:
        held = held + lax.ppermute(held, "gz", [(i, i ^ step) for i in range(blocks)])
        step *= 2
    return held


def on_device(source, cell_width):
    depth, rows, width_x = source.shape
    peers, blocks = lax.axis_size("pa"), lax.axis_size("gz")
    devices = peers * blocks
    width_y = rows * peers
    owned = width_x // devices
    group = LANES // depth
    parts = rows // group

    cosines = halves(cosine_rows(width_x).reshape(owned, devices, width_x))
    order = np.arange(width_y).reshape(peers, parts, group).transpose(1, 0, 2).reshape(-1)
    sines = halves(sine_rows(width_y)[order])
    got = exchange(call_forward(source, *cosines, group), devices)

    own_k = jnp.arange(owned, dtype=jnp.int32) * devices + lax.axis_index(ALL)
    eigen_x, eigen_y = eigen_first(own_k, width_x)[:, None], eigen_second(width_y)[None]
    solve = call_coefficients(all_widths(cell_width, blocks), eigen_x, eigen_y, depth)
    back = call_middle(
        got, *sines, *solve,
        peers=peers, blocks=blocks, depth=depth, parts=parts, group=group, owned=owned,
    )
    return call_backward(exchange(back, devices), *cosines, source.shape, group)


def solution(mesh):
    return jax.shard_map(
        on_device,
        mesh=mesh,
        in_specs=(P("gz", "pa", None), P("gz")),
        out_specs=P("gz", "pa", None),
        check_vma=False,
    )
```

time: 114 us -> 112 us (0.982)
  waiting for transfers between devices: 34.1 us -> 23.1 us
  Pallas kernels: 19.8 us -> 25 us
  starting transfers between devices: 15.6 us -> 19 us
  local copies, waits for them, and re-layouts: 2.23 us -> 1.02 us
    all_to_all x1, waiting for transfers between devices: 34.1 us -> 14.8 us  [exchange(): lax.all_to_all(flat, ALL, split_axis=0, concat_axis=0, tiled=True)]
    ppermute x0 -> x4, waiting for transfers between devices: none -> 8.28 us  [all_widths(): lax.ppermute(held, 'gz', [(i, i ^ step) for i in range(blocks)])]
    pallas_call x3 -> x4, Pallas kernels: 19.8 us -> 25 us  [the longest x1 10.7 us: call_middle(): pl.pallas_call(functools.partial(middle, peers=peers, blocks=blocks, dept...]
    ppermute x0 -> x4, starting transfers between devices: none -> 3.38 us  [all_widths(): lax.ppermute(held, 'gz', [(i, i ^ step) for i in range(blocks)])]
    broadcast_in_dim x1 -> x0, local copies, waits for them, and re-layouts: 1.17 us -> none  [on_device(): widths = jnp.pad(cell_width, (0, LANES - depth))[None]]
  transfers between devices with their start and end apart: 1 -> 5, of which waited for: 1 -> 5; matrix products, arithmetic and copies ran while one was open for 1% -> 2% of each run, Pallas kernels for 0% -> 4%
where the time goes in v1:
time: 112 us; the launch traced here: 111 us
  blocking collectives  40.9 us (37%)
  Pallas kernels  25 us (22%)
  waiting for transfers between devices  23.1 us (21%)
  starting transfers between devices  19 us (17%)
  other arithmetic  2.17 us (2%)
    all_to_all x1, blocking collectives, exchange(): lax.all_to_all(flat, ALL, split_axis=0, concat_axis=0, tiled=True)  40.9 us
    all_to_all x1, starting transfers between devices, exchange(): lax.all_to_all(flat, ALL, split_axis=0, concat_axis=0, tiled=True)  15.6 us
    all_to_all x1, waiting for transfers between devices, exchange(): lax.all_to_all(flat, ALL, split_axis=0, concat_axis=0, tiled=True)  14.8 us
    pallas_call x1, Pallas kernels, call_middle(): pl.pallas_call(functools.partial(middle, peers=peers, blocks=blocks, dept...  10.7 us
    ppermute x4, waiting for transfers between devices, all_widths(): lax.ppermute(held, 'gz', [(i, i ^ step) for i in range(blocks)])  8.28 us
    pallas_call x1, Pallas kernels, call_backward(): pl.pallas_call(functools.partial(backward_x, group=group), name='backward...  5.42 us
    pallas_call x1, Pallas kernels, call_forward(): pl.pallas_call(functools.partial(forward_x, group=group), name='forward_x...  4.82 us
    pallas_call x1, Pallas kernels, call_coefficients(): pl.pallas_call(functools.partial(coefficients, depth=depth, tile=wide //...  4.11 us
  transfers between devices with their start and end apart: 5, of which 5 were waited for; matrix products, arithmetic and copies ran while one was open for 2% of the time, Pallas kernels for 4%

profile of v1, /device:TPU:1, one launch (start us, length us, event | category | flops | bytes accessed | tf_op | source)
XLA Modules:
  0.0 111.3 jit_solution(11578041675434887042)
XLA Ops:
  0.0 4.8 %forward_x.1 = f32[2304,128]{1,0:T(8,128)} custom-call(f32[8,48,768]{2,1,0:T(8,128)} %src_ref.1, bf16[3,256,768]{2,1,0:T(8,128)(2,1)} %constant.32.clone.ch_ref, bf16[3,256,768]{2,1,0:T(8,128)(2,1)} %constant.33.clone.cl_ref), custom_call_target="tpu_custom_call" | custom-call | tf_op jit(solution)/shard_map/forward_x/pallas_call | solution.py:327
  4.8 0.0 copy-start.1
  4.8 15.6 %all-to-all-start = ((f32[256,1,1152]{2,1,0:T(1,128)}), f32[256,1,1152]{2,1,0:T(1,128)S(1)}, u32[]{:S(2)}, u32[]{:S(2)}) async-start(f32[256,1,1152]{2,1,0:T(1,128)} %bitcast.5), calls=%async_computation | async-start | bytes 2359296 | tf_op jit(solution)/shard_map/all_to_all | solution.py:403
  20.5 0.0 copy-done.1
  20.5 0.1 broadcast_select_fusion
  20.6 2.2 %collective-permute-start = (f32[16,128]{1,0:T(8,128)S(1)}, f32[16,128]{1,0:T(8,128)S(1)}, u32[]{:S(2)}, u32[]{:S(2)}) collective-permute-start(f32[16,128]{1,0:T(8,128)S(1)} %broadcast_select_fusion), channel_id=1, source_target_pairs={{0,1},{1,0},{2,3},{3,2},{4,5},{5,4},{6,7},{7,6},{8,9},{9,8},{10,11... | collective-permute-start | bytes 24584 | tf_op jit(solution)/shard_map/ppermute | solution.py:412
  22.8 0.8 collective-permute-done
  23.6 0.1 fusion
  23.7 0.0 collective-permute-start.1
  23.7 2.8 %collective-permute-done.1 = f32[16,128]{1,0:T(8,128)S(1)} collective-permute-done((f32[16,128]{1,0:T(8,128)S(1)}, f32[16,128]{1,0:T(8,128)S(1)}, u32[]{:S(2)}, u32[]{:S(2)}) %collective-permute-start.1) | collective-permute-done | bytes 8224 | tf_op jit(solution)/shard_map/ppermute | solution.py:412
  26.5 0.1 fusion.1
  26.6 1.2 %collective-permute-start.2 = (f32[16,128]{1,0:T(8,128)S(1)}, f32[16,128]{1,0:T(8,128)S(1)}, u32[]{:S(2)}, u32[]{:S(2)}) collective-permute-start(f32[16,128]{1,0:T(8,128)S(1)} %fusion.1), channel_id=1, source_target_pairs={{0,4},{1,5},{2,6},{3,7},{4,0},{5,1},{6,2},{7,3},{8,12},{9,13},{10,... | collective-permute-start | bytes 24584 | tf_op jit(solution)/shard_map/ppermute | solution.py:412
  27.7 0.7 multiply_multiply_fusion.el_ref
  28.4 2.5 %collective-permute-done.2 = f32[16,128]{1,0:T(8,128)S(1)} collective-permute-done((f32[16,128]{1,0:T(8,128)S(1)}, f32[16,128]{1,0:T(8,128)S(1)}, u32[]{:S(2)}, u32[]{:S(2)}) %collective-permute-start.2) | collective-permute-done | bytes 8224 | tf_op jit(solution)/shard_map/ppermute | solution.py:412
  30.9 0.0 collective-permute-start.3
  30.9 0.6 multiply_multiply_fusion.1.ek_ref
  31.6 2.2 %collective-permute-done.3 = f32[16,128]{1,0:T(8,128)S(1)} collective-permute-done((f32[16,128]{1,0:T(8,128)S(1)}, f32[16,128]{1,0:T(8,128)S(1)}, u32[]{:S(2)}, u32[]{:S(2)}) %collective-permute-start.3) | collective-permute-done | bytes 8224 | tf_op jit(solution)/shard_map/ppermute | solution.py:412
  33.8 0.6 add.46.wid_in_ref
  34.4 4.1 %coefficients.1 = (f32[4,384,768]{2,1,0:T(8,128)}, f32[6,384,128]{2,1,0:T(8,128)}) custom-call(f32[16,128]{1,0:T(8,128)} %add.46.wid_in_ref, f32[3,1]{1,0:T(4,128)} %multiply_multiply_fusion.1.ek_ref, f32[1,768]{1,0:T(1,128)} %multiply_multiply_fusion.el_ref), custom_call_target="tpu_custom_call" | custom-call | tf_op jit(solution)/shard_map/coefficients/pallas_call | solution.py:365
  38.5 14.8 %all-to-all-done = f32[256,1,1152]{2,1,0:T(1,128)S(1)} async-done(((f32[256,1,1152]{2,1,0:T(1,128)}), f32[256,1,1152]{2,1,0:T(1,128)S(1)}, u32[]{:S(2)}, u32[]{:S(2)}) %all-to-all-start) | async-done | bytes 1179680 | tf_op jit(solution)/shard_map/all_to_all | solution.py:403
  53.3 1.0 copy-done
  54.3 10.7 %middle.1 = f32[2304,128]{1,0:T(8,128)} custom-call(f32[2304,128]{1,0:T(8,128)} %bitcast.4, bf16[768,768]{1,0:T(8,128)(2,1)} %constant.34.clone.sh_in, bf16[768,768]{1,0:T(8,128)(2,1)} %constant.35.clone.sl_in, f32[4,384,768]{2,1,0:T(8,128)} %get-tuple-element.7.cell_in, f32[6,384,128]{2,1,0:T(8,128)} %get-tuple-element.8.block_in), custom_call_target="tpu_custom_call" | custom-call | tf_op jit(solution)/shard_map/middle/pallas_call | solution.py:381
  65.0 40.9 %all_to_all.10 = f32[256,1,1152]{2,1,0:T(1,128)} all-to-all(f32[256,1,1152]{2,1,0:T(1,128)} %bitcast.6), channel_id=1, replica_groups=mesh['pa'=16,'gz'=16] {'pa','gz'}, dimensions={0} | all-to-all | bytes 2359296 | tf_op jit(solution)/shard_map/all_to_all | solution.py:403
  105.9 5.4 %backward_x.1 = f32[8,48,768]{2,1,0:T(8,128)} custom-call(f32[2304,128]{1,0:T(8,128)} %bitcast.7, bf16[3,256,768]{2,1,0:T(8,128)(2,1)} %constant.32.clone.ch_ref, bf16[3,256,768]{2,1,0:T(8,128)(2,1)} %constant.33.clone.cl_ref), custom_call_target="tpu_custom_call" | custom-call | tf_op jit(solution)/shard_map/backward_x/pallas_call | solution.py:346
  (4 shorter events, 0.0 us)
Async XLA Ops:
  4.8 15.7 %copy-start.1 = (f32[8]{0:T(128)S(1)}, f32[8]{0:T(128)}, u32[]{:S(2)}) copy-start(f32[8]{0:T(128)} %param.7) | copy-start | bytes 100
  4.8 48.4 %all-to-all-start = ((f32[256,1,1152]{2,1,0:T(1,128)}), f32[256,1,1152]{2,1,0:T(1,128)S(1)}, u32[]{:S(2)}, u32[]{:S(2)}) async-start(f32[256,1,1152]{2,1,0:T(1,128)} %bitcast.5), calls=%async_computation | async-start | bytes 2359296 | tf_op jit(solution)/shard_map/all_to_all | solution.py:403
  20.6 3.0 %collective-permute-start = (f32[16,128]{1,0:T(8,128)S(1)}, f32[16,128]{1,0:T(8,128)S(1)}, u32[]{:S(2)}, u32[]{:S(2)}) collective-permute-start(f32[16,128]{1,0:T(8,128)S(1)} %broadcast_select_fusion), channel_id=1, source_target_pairs={{0,1},{1,0},{2,3},{3,2},{4,5},{5,4},{6,7},{7,6},{8,9},{9,8},{10,11... | collective-permute-start | bytes 24584 | tf_op jit(solution)/shard_map/ppermute | solution.py:412
  23.7 2.8 %collective-permute-start.1 = (f32[16,128]{1,0:T(8,128)S(1)}, f32[16,128]{1,0:T(8,128)S(1)}, u32[]{:S(2)}, u32[]{:S(2)}) collective-permute-start(f32[16,128]{1,0:T(8,128)S(1)} %fusion), channel_id=1, source_target_pairs={{0,2},{1,3},{2,0},{3,1},{4,6},{5,7},{6,4},{7,5},{8,10},{9,11},{10,... | collective-permute-start | bytes 24584 | tf_op jit(solution)/shard_map/ppermute | solution.py:412
  26.6 4.3 %collective-permute-start.2 = (f32[16,128]{1,0:T(8,128)S(1)}, f32[16,128]{1,0:T(8,128)S(1)}, u32[]{:S(2)}, u32[]{:S(2)}) collective-permute-start(f32[16,128]{1,0:T(8,128)S(1)} %fusion.1), channel_id=1, source_target_pairs={{0,4},{1,5},{2,6},{3,7},{4,0},{5,1},{6,2},{7,3},{8,12},{9,13},{10,... | collective-permute-start | bytes 24584 | tf_op jit(solution)/shard_map/ppermute | solution.py:412
  30.9 2.8 %collective-permute-start.3 = (f32[16,128]{1,0:T(8,128)S(1)}, f32[16,128]{1,0:T(8,128)S(1)}, u32[]{:S(2)}, u32[]{:S(2)}) collective-permute-start(f32[16,128]{1,0:T(8,128)S(1)} %add.45), channel_id=1, source_target_pairs={{0,8},{1,9},{2,10},{3,11},{4,12},{5,13},{6,14},{7,15},{8,0},{9,1},... | collective-permute-start | bytes 24584 | tf_op jit(solution)/shard_map/ppermute | solution.py:412
  53.3 1.0 copy-start

commit v2 on v1

--- a/solution.py
+++ b/solution.py
@@ -74,35 +74,43 @@
     return blocks
 
 
-def forward_x(src_ref, ch_ref, cl_ref, out_ref, xh_ref, xl_ref, acc_ref, *, group):
-    depth, rows, width = src_ref.shape
+def forward_x(src_ref, ch_ref, cl_ref, out_ref, acc_ref, *, group):
+    depth, rows, some = src_ref.shape
     parts = rows // group
-    owned, some, _ = ch_ref.shape
+    owned, devices, _ = ch_ref.shape
     stride = owned * parts
-
-    @pl.when(pl.program_id(0) == 0)
+    step = pl.program_id(0)
+    x = jnp.concatenate(
+        [src_ref[z, pl.ds(m * group, group), :] for m in range(parts) for z in range(depth)], 0
+    )
+    table = [ref[...].reshape(owned * devices, some) for ref in (ch_ref, cl_ref)]
+    part = dot3(table, split(x), ((1,), (1,)))
+
+    @pl.when(step == 0)
     def _():
-        for m in range(parts):
-            for z in range(depth):
-                at = pl.ds((m * depth + z) * group, group)
-                xh_ref[at, :], xl_ref[at, :] = split(src_ref[z, pl.ds(m * group, group), :])
-
-    table = (ch_ref[...].reshape(owned * some, width), cl_ref[...].reshape(owned * some, width))
-    acc_ref[...] = dot3(table, (xh_ref[...], xl_ref[...]), ((1,), (1,)))
-    for t in range(some // SUB):
-        for kk in range(owned):
-            for m in range(parts):
-                out_ref[pl.ds(t * SUB * stride + kk * parts + m, SUB, stride=stride), :] = acc_ref[
-                    pl.ds(kk * some + t * SUB, SUB), pl.ds(m * LANES, LANES)
-                ]
+        acc_ref[...] = part
+
+    @pl.when(step > 0)
+    def _():
+        acc_ref[...] += part
+
+    @pl.when(step == pl.num_programs(0) - 1)
+    def _():
+        for t in range(devices // SUB):
+            for kk in range(owned):
+                for m in range(parts):
+                    out_ref[pl.ds(t * SUB * stride + kk * parts + m, SUB, stride=stride), :] = acc_ref[
+                        pl.ds(kk * devices + t * SUB, SUB), pl.ds(m * LANES, LANES)
+                    ]
 
 
 def backward_x(msg_ref, ch_ref, cl_ref, out_ref, z_ref, zh_ref, zl_ref, *, group):
-    depth, rows, _ = out_ref.shape
+    depth, rows, some = out_ref.shape
     parts = rows // group
-    owned, devices, some = ch_ref.shape
+    owned, devices, _ = ch_ref.shape
     stride = owned * parts
-    table = [ref[...].reshape(owned * devices, some) for ref in (ch_ref, cl_ref)]
+    cols = pl.ds(pl.multiple_of(pl.program_id(0) * some, some), some)
+    table = [ref[:, :, cols].reshape(owned * devices, some) for ref in (ch_ref, cl_ref)]
 
     @pl.when(pl.program_id(0) == 0)
     def _():
@@ -200,44 +208,49 @@
 
 
 def middle(
-    msg_ref, sh_in, sl_in, cell_in, block_in, out_ref, a_ref, red_ref, sh_ref, sl_ref, cell_ref, block_ref, sems,
+    msg_ref, sh_ref, sl_ref, cell_in, block_in, out_ref, a_ref, xh_ref, xl_ref, red_ref, cell_ref, block_ref, sems,
     *, peers, blocks, depth, parts, group, owned, tile
 ):
     copies = [
         pltpu.make_async_copy(source, target, sems.at[i])
-        for i, (source, target) in enumerate(
-            ((sh_in, sh_ref), (sl_in, sl_ref), (cell_in, cell_ref), (block_in, block_ref))
-        )
+        for i, (source, target) in enumerate(((cell_in, cell_ref), (block_in, block_ref)))
     ]
     for copy in copies:
         copy.start()
-    wide = sh_in.shape[1]
+    wide = sh_ref.shape[1]
     stride = owned * parts
     halfs = peers // depth
     rows = depth * blocks
     cells = wide // LANES
     pitch = -(-owned * cells // SUB) * SUB
 
+    def each(count, body):
+        lax.fori_loop(0, count, lambda i, _: (body(i), 0)[1], 0)
+
     def where(kk, zi):
-        return pl.ds(kk * rows + zi * blocks, blocks)
-
-    for kk in range(owned):
+        return pl.ds(pl.multiple_of(kk * rows + zi * blocks, blocks), blocks)
+
+    def slot(kk, m, g, h):
+        return pl.ds((h * depth + g) * blocks * stride + kk * parts + m, blocks, stride=stride)
+
+    def gather(kk):
         for m in range(parts):
             for h in range(halfs):
-                got = [
-                    msg_ref[pl.ds((h * depth + g) * blocks * stride + kk * parts + m, blocks, stride=stride), :]
-                    for g in range(depth)
-                ]
+                got = [msg_ref[slot(kk, m, g, h), :] for g in range(depth)]
+                lanes = pl.ds((m * halfs + h) * LANES, LANES)
                 for zi, block in enumerate(swap_groups(got, group)):
-                    a_ref[where(kk, zi), pl.ds((m * halfs + h) * LANES, LANES)] = block
-    copies[0].wait()
-    copies[1].wait()
-    table = (sh_ref[...], sl_ref[...])
-    for kk in range(owned):
-        at = pl.ds(kk * rows, rows)
-        a_ref[at, :] = dot3(split(a_ref[at, :]), table, ((1,), (0,)))
-    copies[2].wait()
-    copies[3].wait()
+                    at = where(kk, zi)
+                    xh_ref[at, lanes], xl_ref[at, lanes] = split(block)
+
+    each(owned, gather)
+
+    def transform(j):
+        cols = pl.ds(pl.multiple_of(j * 256, 256), 256)
+        a_ref[:, cols] = dot3((xh_ref[...], xl_ref[...]), (sh_ref[:, cols], sl_ref[:, cols]), ((1,), (0,)))
+
+    each(wide // 256, transform)
+    for copy in copies:
+        copy.wait()
 
     def scatter(index, kk, t, value):
         for s in range(blocks // SUB):
@@ -247,8 +260,7 @@
                     s * SUB : s * SUB + SUB, c * LANES : c * LANES + LANES
                 ]
 
-    red_ref[...] = jnp.zeros(red_ref.shape, jnp.float32)
-    for kk in range(owned):
+    def reduce(kk):
         for t in range(wide // tile):
             cols = pl.ds(t * tile, tile)
             value = [None]
@@ -266,6 +278,9 @@
             at = where(kk, 0)
             scatter(0, kk, t, cell_ref[0, at, cols] * a_ref[at, cols] + cell_ref[1, at, cols] * inner)
             scatter(1, kk, t, value[depth - 1])
+
+    red_ref[...] = jnp.zeros(red_ref.shape, jnp.float32)
+    each(owned, reduce)
 
     rhs = None
     for q in range(blocks):
@@ -286,76 +301,95 @@
         following = red_ref[0, at, :] - block_ref[4, at, :] * tail
         red_ref[0, at, :] = following
 
-    for kk in range(owned):
-        for s in range(blocks // SUB):
-            for c in range(cells):
-                row = s * SUB * pitch + kk * cells + c
-                cols = pl.ds(c * LANES, LANES)
-                for zi, index in ((0, 0), (depth - 1, 1)):
-                    a_ref[pl.ds(kk * rows + zi * blocks + s * SUB, SUB), cols] = red_ref[
-                        index, pl.ds(row, SUB, stride=pitch), :
-                    ]
+    def column(index, kk, t):
+        return jnp.concatenate(
+            [
+                jnp.concatenate(
+                    [
+                        red_ref[index, pl.ds(s * SUB * pitch + kk * cells + t * (tile // LANES) + c, SUB, stride=pitch), :]
+                        for c in range(tile // LANES)
+                    ],
+                    1,
+                )
+                for s in range(blocks // SUB)
+            ],
+            0,
+        )
+
+    def substitute(kk):
         for t in range(wide // tile):
             cols = pl.ds(t * tile, tile)
-            head, following = a_ref[where(kk, 0), cols], a_ref[where(kk, depth - 1), cols]
+            head, following = column(0, kk, t), column(1, kk, t)
+            for zi, value in ((0, head), (depth - 1, following)):
+                at = where(kk, zi)
+                xh_ref[at, cols], xl_ref[at, cols] = split(value)
             for i in range(depth - 2, 0, -1):
                 at = where(kk, i)
                 free = a_ref[at, cols] - cell_ref[2, at, cols] * head
                 following = free - cell_ref[3, at, cols] * following
-                a_ref[at, cols] = following
-        at = pl.ds(kk * rows, rows)
-        a_ref[at, :] = dot3(split(a_ref[at, :]), table, ((1,), (1,)))
+                xh_ref[at, cols], xl_ref[at, cols] = split(following)
+
+    each(owned, substitute)
+
+    def inverse(j):
+        cols = pl.ds(pl.multiple_of(j * 256, 256), 256)
+        a_ref[:, cols] = dot3((xh_ref[...], xl_ref[...]), (sh_ref[cols, :], sl_ref[cols, :]), ((1,), (1,)))
+
+    each(wide // 256, inverse)
+
+    def send(kk):
         for m in range(parts):
             for h in range(halfs):
                 lanes = pl.ds((m * halfs + h) * LANES, LANES)
                 sent = swap_groups([a_ref[where(kk, zi), lanes] for zi in range(depth)], group)
                 for g, block in enumerate(sent):
-                    row = (h * depth + g) * blocks * stride + kk * parts + m
-                    out_ref[pl.ds(row, blocks, stride=stride), :] = block
+                    out_ref[slot(kk, m, g, h), :] = block
+
+    each(owned, send)
 
 
 WHOLE = pl.BlockSpec(memory_space=VMEM)
-STEPS = 2
+PART = 256
+
+
+def on_chip(*arrays):
+    return [pltpu.with_memory_space_constraint(a, VMEM) for a in arrays]
+
+
+def in_hbm(*arrays):
+    return [pltpu.with_memory_space_constraint(a, pltpu.MemorySpace.HBM) for a in arrays]
 
 
 def call_forward(source, high, low, group):
     depth, rows, width = source.shape
-    owned, devices, _ = high.shape
-    some = devices // STEPS
-    table = pl.BlockSpec((owned, some, width), lambda j: (0, j, 0))
-    out = width * depth * rows // LANES
+    table = pl.BlockSpec((*high.shape[:2], PART), lambda j: (0, 0, j))
     return pl.pallas_call(
         functools.partial(forward_x, group=group),
         name="forward_x",
-        grid=(STEPS,),
-        out_shape=jax.ShapeDtypeStruct((out, LANES), jnp.float32),
-        in_specs=[pl.BlockSpec(source.shape, lambda j: (0, 0, 0)), table, table],
-        out_specs=pl.BlockSpec((out // STEPS, LANES), lambda j: (j, 0)),
-        scratch_shapes=[
-            pltpu.VMEM((depth * rows, width), jnp.bfloat16),
-            pltpu.VMEM((depth * rows, width), jnp.bfloat16),
-            pltpu.VMEM((owned * some, depth * rows), jnp.float32),
-        ],
+        grid=(width // PART,),
+        out_shape=pltpu.VMEM((width * depth * rows // LANES, LANES), jnp.float32),
+        in_specs=[pl.BlockSpec((depth, rows, PART), lambda j: (0, 0, j)), table, table],
+        out_specs=WHOLE,
+        scratch_shapes=[pltpu.VMEM((width, depth * rows), jnp.float32)],
     )(source, high, low)
 
 
 def call_backward(message, high, low, shape, group):
     depth, rows, width = shape
-    steps = width // 256
-    table = pl.BlockSpec((*high.shape[:2], width // steps), lambda j: (0, 0, j))
     return pl.pallas_call(
         functools.partial(backward_x, group=group),
         name="backward_x",
-        grid=(steps,),
+        grid=(width // PART,),
         out_shape=jax.ShapeDtypeStruct(shape, jnp.float32),
-        in_specs=[pl.BlockSpec(message.shape, lambda j: (0, 0)), table, table],
-        out_specs=pl.BlockSpec((depth, rows, width // steps), lambda j: (0, 0, j)),
+        in_specs=[WHOLE] * 3,
+        out_specs=pl.BlockSpec((depth, rows, PART), lambda j: (0, 0, j)),
         scratch_shapes=[
             pltpu.VMEM((width, depth * rows), jnp.float32),
             pltpu.VMEM((depth * rows, width), jnp.bfloat16),
             pltpu.VMEM((depth * rows, width), jnp.bfloat16),
         ],
-    )(message, high, low)
+        compiler_params=pltpu.CompilerParams(vmem_limit_bytes=40 * 2**20),
+    )(*on_chip(message, high, low))
 
 
 def call_coefficients(widths, eigen_x, eigen_y, depth):
@@ -377,25 +411,26 @@
 
 def call_middle(message, high, low, cell, block, *, peers, blocks, depth, parts, group, owned):
     wide = high.shape[1]
-    anywhere = pl.BlockSpec(memory_space=pl.ANY)
+    size = (owned * depth * blocks, wide)
     return pl.pallas_call(
         functools.partial(
             middle, peers=peers, blocks=blocks, depth=depth, parts=parts, group=group, owned=owned, tile=wide // 2
         ),
         name="middle",
-        out_shape=jax.ShapeDtypeStruct(message.shape, jnp.float32),
-        in_specs=[WHOLE, *[anywhere] * 4],
+        out_shape=pltpu.VMEM(message.shape, jnp.float32),
+        in_specs=[WHOLE] * 3 + [pl.BlockSpec(memory_space=pltpu.MemorySpace.HBM)] * 2,
         out_specs=WHOLE,
         scratch_shapes=[
-            pltpu.VMEM((owned * depth * blocks, wide), jnp.float32),
+            pltpu.VMEM(size, jnp.float32),
+            pltpu.VMEM(size, jnp.bfloat16),
+            pltpu.VMEM(size, jnp.bfloat16),
             pltpu.VMEM((2, *block.shape[1:]), jnp.float32),
-            pltpu.VMEM(high.shape, jnp.bfloat16),
-            pltpu.VMEM(low.shape, jnp.bfloat16),
             pltpu.VMEM(cell.shape, jnp.float32),
             pltpu.VMEM(block.shape, jnp.float32),
-            pltpu.SemaphoreType.DMA((4,)),
+            pltpu.SemaphoreType.DMA((2,)),
         ],
-    )(message, high, low, cell, block)
+        compiler_params=pltpu.CompilerParams(vmem_limit_bytes=40 * 2**20),
+    )(*on_chip(message, high, low), *in_hbm(cell, block))
 
 
 def exchange(rows, devices):

time: 112 us -> 106 us (0.946)
  Pallas kernels: 25 us -> 21.4 us
    pallas_call x1, Pallas kernels: 5.42 us -> 3.23 us  [call_backward(): pl.pallas_call(functools.partial(backward_x, group=group), name='backward...]
    pallas_call x1, Pallas kernels: 10.7 us -> 8.74 us  [call_middle(): pl.pallas_call(functools.partial(middle, peers=peers, blocks=blocks, dept...]
where the time goes in v2:
time: 106 us
  blocking collectives  40 us (38%)
  waiting for transfers between devices  23.1 us (22%)
  Pallas kernels  21.4 us (20%)
  starting transfers between devices  19 us (18%)
  other arithmetic  2.17 us (2%)
    all_to_all x1, blocking collectives, exchange(): lax.all_to_all(flat, ALL, split_axis=0, concat_axis=0, tiled=True)  40 us
    all_to_all x1, starting transfers between devices, exchange(): lax.all_to_all(flat, ALL, split_axis=0, concat_axis=0, tiled=True)  15.7 us
    all_to_all x1, waiting for transfers between devices, exchange(): lax.all_to_all(flat, ALL, split_axis=0, concat_axis=0, tiled=True)  14.8 us
    pallas_call x1, Pallas kernels, call_middle(): pl.pallas_call(functools.partial(middle, peers=peers, blocks=blocks, dept...  8.74 us
    ppermute x4, waiting for transfers between devices, all_widths(): lax.ppermute(held, 'gz', [(i, i ^ step) for i in range(blocks)])  8.28 us
    pallas_call x1, Pallas kernels, call_forward(): pl.pallas_call(functools.partial(forward_x, group=group), name='forward_x...  5.35 us
    pallas_call x1, Pallas kernels, call_coefficients(): pl.pallas_call(functools.partial(coefficients, depth=depth, tile=wide //...  4.11 us
    ppermute x4, starting transfers between devices, all_widths(): lax.ppermute(held, 'gz', [(i, i ^ step) for i in range(blocks)])  3.38 us
  transfers between devices with their start and end apart: 5, of which 5 were waited for; matrix products, arithmetic and copies ran while one was open for 2% of the time, Pallas kernels for 4%

profile of v2, /device:TPU:1, one launch (start us, length us, event | category | flops | bytes accessed | tf_op | source)
XLA Modules:
  0.0 105.8 jit_solution(11678399986016311994)
XLA Ops:
  0.0 5.4 %forward_x.1 = f32[2304,128]{1,0:T(8,128)} custom-call(f32[8,48,768]{2,1,0:T(8,128)} %src_ref.1, bf16[3,256,768]{2,1,0:T(8,128)(2,1)} %constant.32.clone.ch_ref, bf16[3,256,768]{2,1,0:T(8,128)(2,1)} %constant.33.clone.cl_ref), custom_call_target="tpu_custom_call" | custom-call | tf_op jit(solution)/shard_map/forward_x/pallas_call | solution.py:366
  5.4 15.7 %all-to-all-start = ((f32[256,1,1152]{2,1,0:T(1,128)}), f32[256,1,1152]{2,1,0:T(1,128)S(1)}, u32[]{:S(2)}, u32[]{:S(2)}) async-start(f32[256,1,1152]{2,1,0:T(1,128)} %bitcast), calls=%async_computation | async-start | bytes 2359296 | tf_op jit(solution)/shard_map/all_to_all | solution.py:438
  21.0 0.0 copy-done.4
  21.1 0.1 broadcast_select_fusion
  21.1 2.2 %collective-permute-start = (f32[16,128]{1,0:T(8,128)S(1)}, f32[16,128]{1,0:T(8,128)S(1)}, u32[]{:S(2)}, u32[]{:S(2)}) collective-permute-start(f32[16,128]{1,0:T(8,128)S(1)} %broadcast_select_fusion), channel_id=1, source_target_pairs={{0,1},{1,0},{2,3},{3,2},{4,5},{5,4},{6,7},{7,6},{8,9},{9,8},{10,11... | collective-permute-start | bytes 24584 | tf_op jit(solution)/shard_map/ppermute | solution.py:447
  23.3 0.8 collective-permute-done
  24.1 0.1 fusion
  24.2 0.0 collective-permute-start.1
  24.2 2.8 %collective-permute-done.1 = f32[16,128]{1,0:T(8,128)S(1)} collective-permute-done((f32[16,128]{1,0:T(8,128)S(1)}, f32[16,128]{1,0:T(8,128)S(1)}, u32[]{:S(2)}, u32[]{:S(2)}) %collective-permute-start.1) | collective-permute-done | bytes 8224 | tf_op jit(solution)/shard_map/ppermute | solution.py:447
  27.0 0.1 fusion.1
  27.1 1.2 %collective-permute-start.2 = (f32[16,128]{1,0:T(8,128)S(1)}, f32[16,128]{1,0:T(8,128)S(1)}, u32[]{:S(2)}, u32[]{:S(2)}) collective-permute-start(f32[16,128]{1,0:T(8,128)S(1)} %fusion.1), channel_id=1, source_target_pairs={{0,4},{1,5},{2,6},{3,7},{4,0},{5,1},{6,2},{7,3},{8,12},{9,13},{10,... | collective-permute-start | bytes 24584 | tf_op jit(solution)/shard_map/ppermute | solution.py:447
  28.3 0.7 multiply_multiply_fusion.el_ref
  29.0 2.5 %collective-permute-done.2 = f32[16,128]{1,0:T(8,128)S(1)} collective-permute-done((f32[16,128]{1,0:T(8,128)S(1)}, f32[16,128]{1,0:T(8,128)S(1)}, u32[]{:S(2)}, u32[]{:S(2)}) %collective-permute-start.2) | collective-permute-done | bytes 8224 | tf_op jit(solution)/shard_map/ppermute | solution.py:447
  31.5 0.0 collective-permute-start.3
  31.5 0.6 multiply_multiply_fusion.1.ek_ref
  32.1 2.2 %collective-permute-done.3 = f32[16,128]{1,0:T(8,128)S(1)} collective-permute-done((f32[16,128]{1,0:T(8,128)S(1)}, f32[16,128]{1,0:T(8,128)S(1)}, u32[]{:S(2)}, u32[]{:S(2)}) %collective-permute-start.3) | collective-permute-done | bytes 8224 | tf_op jit(solution)/shard_map/ppermute | solution.py:447
  34.3 0.6 add.46.wid_in_ref
  34.9 4.1 %coefficients.1 = (f32[4,384,768]{2,1,0:T(8,128)}, f32[6,384,128]{2,1,0:T(8,128)}) custom-call(f32[16,128]{1,0:T(8,128)} %add.46.wid_in_ref, f32[3,1]{1,0:T(4,128)} %multiply_multiply_fusion.1.ek_ref, f32[1,768]{1,0:T(1,128)} %multiply_multiply_fusion.el_ref), custom_call_target="tpu_custom_call" | custom-call | tf_op jit(solution)/shard_map/coefficients/pallas_call | solution.py:399
  39.0 14.8 %all-to-all-done = f32[256,1,1152]{2,1,0:T(1,128)S(1)} async-done(((f32[256,1,1152]{2,1,0:T(1,128)}), f32[256,1,1152]{2,1,0:T(1,128)S(1)}, u32[]{:S(2)}, u32[]{:S(2)}) %all-to-all-start) | async-done | bytes 1179680 | tf_op jit(solution)/shard_map/all_to_all | solution.py:438
  53.8 8.7 %middle.1 = f32[2304,128]{1,0:T(8,128)S(1)} custom-call(f32[2304,128]{1,0:T(8,128)S(1)} %bitcast.4, bf16[768,768]{1,0:T(8,128)(2,1)S(1)} %copy-done.3, bf16[768,768]{1,0:T(8,128)(2,1)S(1)} %copy-done.2, f32[4,384,768]{2,1,0:T(8,128)} %get-tuple-element.7.cell_in, f32[6,384,128]{2,1,0:T(8,128)} %get-tuple-element.8.block_in), custom_call_target="tpu_custom_call" | custom-call | tf_op jit(solution)/shard_map/middle/pallas_call | solution.py:415
  62.6 0.0 copy-start
  62.6 0.0 copy-start.1
  62.6 40.0 %all_to_all.10 = f32[256,1,1152]{2,1,0:T(1,128)S(1)} all-to-all(f32[256,1,1152]{2,1,0:T(1,128)S(1)} %bitcast.5), channel_id=1, replica_groups=mesh['pa'=16,'gz'=16] {'pa','gz'}, dimensions={0} | all-to-all | bytes 2359296 | tf_op jit(solution)/shard_map/all_to_all | solution.py:438
  102.6 3.2 %backward_x.1 = f32[8,48,768]{2,1,0:T(8,128)} custom-call(f32[2304,128]{1,0:T(8,128)S(1)} %bitcast.6, bf16[3,256,768]{2,1,0:T(8,128)(2,1)S(1)} %copy-done.1, bf16[3,256,768]{2,1,0:T(8,128)(2,1)S(1)} %copy-done), custom_call_target="tpu_custom_call" | custom-call | tf_op jit(solution)/shard_map/backward_x/pallas_call | solution.py:379
  (10 shorter events, 0.0 us)
Async XLA Ops:
  5.4 15.7 %copy-start.4 = (f32[8]{0:T(128)S(1)}, f32[8]{0:T(128)}, u32[]{:S(2)}) copy-start(f32[8]{0:T(128)} %param.7) | copy-start | bytes 100
  5.4 48.5 %copy-start.2 = (bf16[768,768]{1,0:T(8,128)(2,1)S(1)}, bf16[768,768]{1,0:T(8,128)(2,1)}, u32[]{:S(2)}) copy-start(bf16[768,768]{1,0:T(8,128)(2,1)} %constant.35.clone.sl_ref) | copy-start | bytes 3538948
  5.4 48.5 %copy-start.3 = (bf16[768,768]{1,0:T(8,128)(2,1)S(1)}, bf16[768,768]{1,0:T(8,128)(2,1)}, u32[]{:S(2)}) copy-start(bf16[768,768]{1,0:T(8,128)(2,1)} %constant.34.clone.sh_ref) | copy-start | bytes 3538948
  5.4 48.5 %all-to-all-start = ((f32[256,1,1152]{2,1,0:T(1,128)}), f32[256,1,1152]{2,1,0:T(1,128)S(1)}, u32[]{:S(2)}, u32[]{:S(2)}) async-start(f32[256,1,1152]{2,1,0:T(1,128)} %bitcast), calls=%async_computation | async-start | bytes 2359296 | tf_op jit(solution)/shard_map/all_to_all | solution.py:438
  21.1 3.0 %collective-permute-start = (f32[16,128]{1,0:T(8,128)S(1)}, f32[16,128]{1,0:T(8,128)S(1)}, u32[]{:S(2)}, u32[]{:S(2)}) collective-permute-start(f32[16,128]{1,0:T(8,128)S(1)} %broadcast_select_fusion), channel_id=1, source_target_pairs={{0,1},{1,0},{2,3},{3,2},{4,5},{5,4},{6,7},{7,6},{8,9},{9,8},{10,11... | collective-permute-start | bytes 24584 | tf_op jit(solution)/shard_map/ppermute | solution.py:447
  24.2 2.8 %collective-permute-start.1 = (f32[16,128]{1,0:T(8,128)S(1)}, f32[16,128]{1,0:T(8,128)S(1)}, u32[]{:S(2)}, u32[]{:S(2)}) collective-permute-start(f32[16,128]{1,0:T(8,128)S(1)} %fusion), channel_id=1, source_target_pairs={{0,2},{1,3},{2,0},{3,1},{4,6},{5,7},{6,4},{7,5},{8,10},{9,11},{10,... | collective-permute-start | bytes 24584 | tf_op jit(solution)/shard_map/ppermute | solution.py:447
  27.1 4.3 %collective-permute-start.2 = (f32[16,128]{1,0:T(8,128)S(1)}, f32[16,128]{1,0:T(8,128)S(1)}, u32[]{:S(2)}, u32[]{:S(2)}) collective-permute-start(f32[16,128]{1,0:T(8,128)S(1)} %fusion.1), channel_id=1, source_target_pairs={{0,4},{1,5},{2,6},{3,7},{4,0},{5,1},{6,2},{7,3},{8,12},{9,13},{10,... | collective-permute-start | bytes 24584 | tf_op jit(solution)/shard_map/ppermute | solution.py:447
  31.5 2.8 %collective-permute-start.3 = (f32[16,128]{1,0:T(8,128)S(1)}, f32[16,128]{1,0:T(8,128)S(1)}, u32[]{:S(2)}, u32[]{:S(2)}) collective-permute-start(f32[16,128]{1,0:T(8,128)S(1)} %add.45), channel_id=1, source_target_pairs={{0,8},{1,9},{2,10},{3,11},{4,12},{5,13},{6,14},{7,15},{8,0},{9,1},... | collective-permute-start | bytes 24584 | tf_op jit(solution)/shard_map/ppermute | solution.py:447
  62.6 40.0 %copy-start = (bf16[3,256,768]{2,1,0:T(8,128)(2,1)S(1)}, bf16[3,256,768]{2,1,0:T(8,128)(2,1)}, u32[]{:S(2)}) copy-start(bf16[3,256,768]{2,1,0:T(8,128)(2,1)} %constant.33.clone.cl_ref) | copy-start | bytes 3538948
  62.6 40.0 %copy-start.1 = (bf16[3,256,768]{2,1,0:T(8,128)(2,1)S(1)}, bf16[3,256,768]{2,1,0:T(8,128)(2,1)}, u32[]{:S(2)}) copy-start(bf16[3,256,768]{2,1,0:T(8,128)(2,1)} %constant.32.clone.ch_ref) | copy-start | bytes 3538948

commit v3 on v2

v3 whole, which is shorter than its diff:
```python
import functools
import math

import numpy as np

import jax
import jax.numpy as jnp
from jax import lax
from jax.experimental import pallas as pl
from jax.experimental.pallas import tpu as pltpu
from jax.sharding import PartitionSpec as P

ALL = ("pa", "gz")
LANES = 128
SUB = 8
VMEM = pltpu.MemorySpace.VMEM


def halves(table):
    table = table.astype(np.float32)
    high = table.astype(jnp.bfloat16)
    low = (table - high.astype(np.float32)).astype(jnp.bfloat16)
    return jnp.asarray(high), jnp.asarray(low)


def cosine_rows(width):
    k = np.arange(width)
    phases = k[:, None] * (2 * k[None, :] + 1) % (4 * width)
    weights = np.where(k == 0, math.sqrt(1.0 / width), math.sqrt(2.0 / width))
    return weights[:, None] * np.cos(phases * (math.pi / (2 * width)))


def sine_rows(width):
    k = np.arange(1, width + 1)
    phases = k[:, None] * k[None, :] % (2 * (width + 1))
    return math.sqrt(2.0 / (width + 1)) * np.sin(phases * (math.pi / (width + 1)))


def order_y(values, peers, parts, group):
    return values.reshape(peers, parts, group).transpose(1, 0, 2).reshape(-1)


def sine_tables(peers, parts, group):
    width = peers * parts * group
    order = order_y(np.arange(width), peers, parts, group)
    return halves(sine_rows(width)[order][:, order])


def eigen_first(wavenumber, width):
    return 4.0 * jnp.square(jnp.sin(wavenumber.astype(jnp.float32) * (math.pi / (2 * width))))


def eigen_second(index, width):
    wavenumber = (index + 1).astype(jnp.float32)
    return 4.0 * jnp.square(jnp.sin(wavenumber * (math.pi / (2 * (width + 1)))))


def split(x):
    high = x.astype(jnp.bfloat16)
    return high, (x - high.astype(jnp.float32)).astype(jnp.bfloat16)


def dot3(a, b, dims):
    lhs = jnp.concatenate([a[0], a[1], a[0]], dims[0][0])
    rhs = jnp.concatenate([b[0], b[0], b[1]], dims[1][0])
    return lax.dot_general(lhs, rhs, (dims, ((), ())), preferred_element_type=jnp.float32)


def swap_groups(blocks, group):
    n = len(blocks)
    lanes = n * group
    lane = lax.broadcasted_iota(jnp.int32, blocks[0].shape, 1)
    blocks = list(blocks)
    d = 1
    while d < n:
        keep = (lane & (d * group)) == 0
        for i in range(n):
            if i & d:
                continue
            a, b = blocks[i], blocks[i + d]
            blocks[i] = jnp.where(keep, a, pltpu.roll(b, d * group, 1))
            blocks[i + d] = jnp.where(keep, pltpu.roll(a, lanes - d * group, 1), b)
        d *= 2
    return blocks


def mirrored(x):
    tiles = x.shape[1] // LANES
    lane = lax.broadcasted_iota(jnp.int32, (x.shape[0], LANES), 1)
    parts = [x[:, c * LANES : c * LANES + LANES] for c in range(tiles)]
    return jnp.concatenate([jnp.take_along_axis(p, LANES - 1 - lane, 1) for p in parts[::-1]], 1)


def start_copies(pairs, sems):
    copies = [pltpu.make_async_copy(a, b, sems.at[i]) for i, (a, b) in enumerate(pairs)]
    for copy in copies:
        copy.start()
    return copies


def forward_x(src_ref, ch_in, cl_in, out_ref, acc_ref, ch_ref, cl_ref, sems, *, owned, group):
    copies = start_copies(((ch_in, ch_ref), (cl_in, cl_ref)), sems)
    depth, rows, width = src_ref.shape
    parts = rows // group
    half = width // 2
    each = half // owned
    stride = owned * parts
    x = jnp.concatenate(
        [src_ref[z, pl.ds(m * group, group), :] for m in range(parts) for z in range(depth)], 0
    )
    near, far = x[:, :half], mirrored(x[:, half:])
    folded = split(near + far), split(near - far)
    for copy in copies:
        copy.wait()
    for odd in range(2):
        at = pl.ds(odd * half, half)
        acc_ref[at, :] = dot3((ch_ref[at, :], cl_ref[at, :]), folded[odd], ((1,), (1,)))
        for t in range(each // SUB):
            for kk in range(owned):
                for m in range(parts):
                    row = (odd + 2 * SUB * t) * stride + kk * parts + m
                    out_ref[pl.ds(row, SUB, stride=2 * stride), :] = acc_ref[
                        pl.ds(odd * half + kk * each + t * SUB, SUB), pl.ds(m * LANES, LANES)
                    ]


def backward_x(msg_ref, ch_ref, cl_ref, out_ref, z_ref, y_ref, part_ref, sems, *, owned, group):
    depth, rows, width = out_ref.shape
    parts = rows // group
    half = width // 2
    each = half // owned
    stride = owned * parts
    for odd in range(2):
        for t in range(each // SUB):
            for kk in range(owned):
                for m in range(parts):
                    row = (odd + 2 * SUB * t) * stride + kk * parts + m
                    z_ref[pl.ds(odd * half + kk * each + t * SUB, SUB), pl.ds(m * LANES, LANES)] = msg_ref[
                        pl.ds(row, SUB, stride=2 * stride), :
                    ]
    for odd in range(2):
        at = pl.ds(odd * half, half)
        y_ref[odd] = dot3(split(z_ref[at, :].T), (ch_ref[at, :], cl_ref[at, :]), ((1,), (0,)))
    copies = []
    for m in range(parts):
        at = pl.ds(m * depth * group, depth * group)
        even, odd = y_ref[0, at, :], y_ref[1, at, :]
        near, far = even + odd, mirrored(even - odd)
        for z in range(depth):
            part_ref[z, pl.ds(m * group, group), pl.ds(0, half)] = near[z * group : z * group + group]
            part_ref[z, pl.ds(m * group, group), pl.ds(half, half)] = far[z * group : z * group + group]
        where = (slice(None), pl.ds(m * group, group), slice(None))
        copies.append(pltpu.make_async_copy(part_ref.at[where], out_ref.at[where], sems.at[m]))
        copies[-1].start()
    for copy in copies:
        copy.wait()


def coefficients(wid_in_ref, ek_ref, el_ref, cell_ref, link_ref, block_ref, wid_ref, red_ref, *, depth, tile):
    blocks = wid_in_ref.shape[0]
    owned, wide = ek_ref.shape[0], el_ref.shape[1]
    rows = depth * blocks
    cells = wide // LANES
    pitch = -(-owned * cells // SUB) * SUB

    wid_ref[...] = jnp.zeros(wid_ref.shape, jnp.float32)
    wid_ref[pl.ds(SUB, blocks), :] = wid_in_ref[...]
    width = wid_ref[pl.ds(SUB, blocks), :]
    before, after = wid_ref[pl.ds(SUB - 1, blocks), :], wid_ref[pl.ds(SUB + 1, blocks), :]
    column = lambda a, i: a[:, i : i + 1]
    width_of = [column(width, i) for i in range(depth)]
    padded = [column(before, depth - 1), *width_of, column(after, 0)]
    link = [2.0 / (padded[i] + padded[i + 1]) for i in range(depth + 1)]
    lower, upper = link[:-1], link[1:]
    red_ref[...] = jnp.zeros(red_ref.shape, jnp.float32)
    for i in range(depth):
        for index, value in ((0, upper[0] if i == 0 else lower[i]), (1, -upper[i])):
            link_ref[index, pl.ds(i * blocks, blocks), :] = jnp.broadcast_to(value / width_of[i], (blocks, LANES))

    def scatter(index, kk, t, value):
        for s in range(blocks // SUB):
            for c in range(tile // LANES):
                row = s * SUB * pitch + kk * cells + t * (tile // LANES) + c
                red_ref[index, pl.ds(row, SUB, stride=pitch), :] = value[
                    s * SUB : s * SUB + SUB, c * LANES : c * LANES + LANES
                ]

    for kk in range(owned):
        for t in range(wide // tile):
            cols = pl.ds(t * tile, tile)
            eigen = ek_ref[kk : kk + 1, :] + el_ref[:, cols]
            diagonal = lambda i: (lower[i] + upper[i]) + width_of[i] * eigen
            left, right = [None], [None]
            for i in range(1, depth):
                if i == 1:
                    inverse = 1.0 / diagonal(i)
                    left.append(-(inverse * lower[i]))
                else:
                    inverse = 1.0 / (diagonal(i) + lower[i] * right[-1])
                    left.append(inverse * lower[i] * left[-1])
                right.append(-(inverse * upper[i]))
                at = pl.ds(kk * rows + i * blocks, blocks)
                cell_ref[0, at, cols] = inverse * width_of[i]
                cell_ref[1, at, cols] = left[i]
            inner_left, inner_right = left[depth - 2], right[depth - 2]
            for i in range(depth - 3, 0, -1):
                inner_left = left[i] - right[i] * inner_left
                inner_right = -(right[i] * inner_right)
            inverse = 1.0 / (diagonal(0) + upper[0] * inner_left)
            at = pl.ds(kk * rows, blocks)
            cell_ref[0, at, cols] = inverse * width_of[0]
            cell_ref[1, at, cols] = jnp.zeros(inverse.shape, jnp.float32)
            scatter(0, kk, t, -(inverse * lower[0]))
            scatter(1, kk, t, inverse * upper[0] * inner_right)
            scatter(2, kk, t, left[depth - 1])
            scatter(3, kk, t, right[depth - 1])

    ratio = None
    for q in range(blocks):
        at = pl.ds(q * pitch, pitch)
        head_below, head_above, tail_below, tail_above = (red_ref[i, at, :] for i in range(4))
        if q == 0:
            head_own = jnp.ones(head_above.shape, jnp.float32)
            head_up = jnp.zeros(head_above.shape, jnp.float32)
            head_ratio = head_above
        else:
            head_own = 1.0 / (1.0 - head_below * ratio)
            head_up = -(head_below * head_own)
            head_ratio = head_above * head_own
        tail_own = 1.0 / (1.0 - tail_below * head_ratio)
        ratio = tail_above * tail_own
        found = (head_own, head_up, tail_own, -(tail_below * tail_own), head_ratio, ratio)
        for index, value in enumerate(found):
            block_ref[index, at, :] = value


def middle(
    msg_ref, sh_ref, sl_ref, cell_in, link_in, block_in, out_ref, a_ref, xh_ref, xl_ref, red_ref, cell_ref, link_ref,
    block_ref, sems, *, peers, blocks, depth, parts, group, owned, tile
):
    copies = start_copies(
        ((cell_in, cell_ref), (link_in, link_ref), (block_in, block_ref)), sems
    )
    wide = sh_ref.shape[1]
    stride = owned * parts
    halfs = peers // depth
    rows = depth * blocks
    cells = wide // LANES
    pitch = -(-owned * cells // SUB) * SUB

    def where(kk, zi):
        return pl.ds(kk * rows + zi * blocks, blocks)

    def slot(kk, m, g, h):
        return pl.ds((h * depth + g) * blocks * stride + kk * parts + m, blocks, stride=stride)

    def gather(m, h):
        got = [
            jnp.concatenate([msg_ref[slot(kk, m, g, h), :] for kk in range(owned)], 0) for g in range(depth)
        ]
        lanes = pl.ds((m * halfs + h) * LANES, LANES)
        for zi, block in enumerate(swap_groups(got, group)):
            high, low = split(block)
            for kk in range(owned):
                at = where(kk, zi)
                xh_ref[at, lanes] = high[kk * blocks : kk * blocks + blocks]
                xl_ref[at, lanes] = low[kk * blocks : kk * blocks + blocks]

    for m in range(parts):
        for h in range(halfs):
            gather(m, h)
        at = pl.ds(m * halfs * LANES, halfs * LANES)
        part = dot3((xh_ref[:, at], xl_ref[:, at]), (sh_ref[at, :], sl_ref[at, :]), ((1,), (0,)))
        if m == 0:
            a_ref[...] = part
        else:
            a_ref[...] += part
    for copy in copies:
        copy.wait()
    link = lambda index, i: jnp.concatenate([link_ref[index, pl.ds(i * blocks, blocks), :]] * (tile // LANES), 1)

    def scatter(index, kk, t, value):
        for s in range(blocks // SUB):
            for c in range(tile // LANES):
                row = s * SUB * pitch + kk * cells + t * (tile // LANES) + c
                red_ref[index, pl.ds(row, SUB, stride=pitch), :] = value[
                    s * SUB : s * SUB + SUB, c * LANES : c * LANES + LANES
                ]

    def reduce(kk):
        for t in range(wide // tile):
            cols = pl.ds(t * tile, tile)
            value = [None]
            for i in range(1, depth):
                at = where(kk, i)
                now = a_ref[at, cols]
                if i > 1:
                    now = now + link(0, i) * value[-1]
                value.append(cell_ref[0, at, cols] * now)
                if i < depth - 1:
                    a_ref[at, cols] = value[i]
            inner = value[depth - 2]
            for i in range(depth - 3, 0, -1):
                inner = value[i] - cell_ref[0, where(kk, i), cols] * (link(1, i) * inner)
            at = where(kk, 0)
            scatter(0, kk, t, cell_ref[0, at, cols] * (a_ref[at, cols] + link(0, 0) * inner))
            scatter(1, kk, t, value[depth - 1])

    red_ref[...] = jnp.zeros(red_ref.shape, jnp.float32)
    for kk in range(owned):
        reduce(kk)

    rhs = None
    for q in range(blocks):
        at = pl.ds(q * pitch, pitch)
        head = block_ref[0, at, :] * red_ref[0, at, :]
        if rhs is not None:
            head = head + block_ref[1, at, :] * rhs
        rhs = block_ref[2, at, :] * red_ref[1, at, :] + block_ref[3, at, :] * head
        red_ref[0, at, :] = head
        red_ref[1, at, :] = rhs
    following = None
    for q in range(blocks - 1, -1, -1):
        at = pl.ds(q * pitch, pitch)
        tail = red_ref[1, at, :]
        if following is not None:
            tail = tail - block_ref[5, at, :] * following
            red_ref[1, at, :] = tail
        following = red_ref[0, at, :] - block_ref[4, at, :] * tail
        red_ref[0, at, :] = following

    def column(index, kk, t):
        return jnp.concatenate(
            [
                jnp.concatenate(
                    [
                        red_ref[index, pl.ds(s * SUB * pitch + kk * cells + t * (tile // LANES) + c, SUB, stride=pitch), :]
                        for c in range(tile // LANES)
                    ],
                    1,
                )
                for s in range(blocks // SUB)
            ],
            0,
        )

    def substitute(kk):
        for t in range(wide // tile):
            cols = pl.ds(t * tile, tile)
            head, following = column(0, kk, t), column(1, kk, t)
            for zi, value in ((0, head), (depth - 1, following)):
                at = where(kk, zi)
                xh_ref[at, cols], xl_ref[at, cols] = split(value)
            for i in range(depth - 2, 0, -1):
                at = where(kk, i)
                free = a_ref[at, cols] - cell_ref[1, at, cols] * head
                following = free - cell_ref[0, at, cols] * (link(1, i) * following)
                xh_ref[at, cols], xl_ref[at, cols] = split(following)

    for kk in range(owned):
        substitute(kk)

    def send(m, h):
        lanes = pl.ds((m * halfs + h) * LANES, LANES)
        sent = swap_groups(
            [jnp.concatenate([a_ref[where(kk, zi), lanes] for kk in range(owned)], 0) for zi in range(depth)], group
        )
        for g, block in enumerate(sent):
            for kk in range(owned):
                out_ref[slot(kk, m, g, h), :] = block[kk * blocks : kk * blocks + blocks]

    for m in range(parts):
        at = pl.ds(m * halfs * LANES, halfs * LANES)
        a_ref[:, at] = dot3((xh_ref[...], xl_ref[...]), (sh_ref[:, at], sl_ref[:, at]), ((1,), (0,)))
        for h in range(halfs):
            send(m, h)


WHOLE = pl.BlockSpec(memory_space=VMEM)
PART = 256


def on_chip(*arrays):
    return [pltpu.with_memory_space_constraint(a, VMEM) for a in arrays]


def in_hbm(*arrays):
    return [pltpu.with_memory_space_constraint(a, pltpu.MemorySpace.HBM) for a in arrays]


HBM = pl.BlockSpec(memory_space=pltpu.MemorySpace.HBM)


def call_forward(source, high, low, owned, group):
    depth, rows, width = source.shape
    return pl.pallas_call(
        functools.partial(forward_x, owned=owned, group=group),
        name="forward_x",
        out_shape=pltpu.VMEM((width * depth * rows // LANES, LANES), jnp.float32),
        in_specs=[WHOLE, HBM, HBM],
        out_specs=WHOLE,
        scratch_shapes=[
            pltpu.VMEM((width, depth * rows), jnp.float32),
            pltpu.VMEM(high.shape, jnp.bfloat16),
            pltpu.VMEM(low.shape, jnp.bfloat16),
            pltpu.SemaphoreType.DMA((2,)),
        ],
    )(source, *in_hbm(high, low))


def call_backward(message, high, low, shape, owned, group):
    depth, rows, width = shape
    return pl.pallas_call(
        functools.partial(backward_x, owned=owned, group=group),
        name="backward_x",
        out_shape=jax.ShapeDtypeStruct(shape, jnp.float32),
        in_specs=[WHOLE] * 3,
        out_specs=HBM,
        scratch_shapes=[
            pltpu.VMEM((width, depth * rows), jnp.float32),
            pltpu.VMEM((2, depth * rows, width // 2), jnp.float32),
            pltpu.VMEM(shape, jnp.float32),
            pltpu.SemaphoreType.DMA((rows // group,)),
        ],
        compiler_params=pltpu.CompilerParams(vmem_limit_bytes=40 * 2**20),
    )(*on_chip(message, high, low))


def call_coefficients(widths, eigen_x, eigen_y, depth):
    blocks, owned, wide = widths.shape[0], eigen_x.shape[0], eigen_y.shape[1]
    pitch = -(-owned * (wide // LANES) // SUB) * SUB
    shapes = ((2, owned * depth * blocks, wide), (2, depth * blocks, LANES), (6, blocks * pitch, LANES))
    return pl.pallas_call(
        functools.partial(coefficients, depth=depth, tile=wide // 2),
        name="coefficients",
        out_shape=[jax.ShapeDtypeStruct(s, jnp.float32) for s in shapes],
        in_specs=[WHOLE] * 3,
        out_specs=[WHOLE] * 3,
        scratch_shapes=[
            pltpu.VMEM((blocks + 2 * SUB, LANES), jnp.float32),
            pltpu.VMEM((4, blocks * pitch, LANES), jnp.float32),
        ],
    )(widths, eigen_x, eigen_y)


def call_middle(message, high, low, cell, link, block, *, peers, blocks, depth, parts, group, owned):
    wide = high.shape[1]
    size = (owned * depth * blocks, wide)
    return pl.pallas_call(
        functools.partial(
            middle, peers=peers, blocks=blocks, depth=depth, parts=parts, group=group, owned=owned, tile=wide // 2
        ),
        name="middle",
        out_shape=pltpu.VMEM(message.shape, jnp.float32),
        in_specs=[WHOLE] * 3 + [HBM] * 3,
        out_specs=WHOLE,
        scratch_shapes=[
            pltpu.VMEM(size, jnp.float32),
            pltpu.VMEM(size, jnp.bfloat16),
            pltpu.VMEM(size, jnp.bfloat16),
            pltpu.VMEM((2, *block.shape[1:]), jnp.float32),
            pltpu.VMEM(cell.shape, jnp.float32),
            pltpu.VMEM(link.shape, jnp.float32),
            pltpu.VMEM(block.shape, jnp.float32),
            pltpu.SemaphoreType.DMA((3,)),
        ],
        compiler_params=pltpu.CompilerParams(vmem_limit_bytes=40 * 2**20),
    )(*on_chip(message, high, low), *in_hbm(cell, link, block))


def exchange(rows, devices):
    flat = rows.reshape(devices, 1, -1)
    return lax.all_to_all(flat, ALL, split_axis=0, concat_axis=0, tiled=True).reshape(-1, LANES)


def all_widths(cell_width, blocks):
    depth = cell_width.shape[0]
    row = lax.broadcasted_iota(jnp.int32, (blocks, LANES), 0)
    held = jnp.where(row == lax.axis_index("gz"), jnp.pad(cell_width, (0, LANES - depth))[None], 0.0)
    step = 1
    while step < blocks:
        held = held + lax.ppermute(held, "gz", [(i, i ^ step) for i in range(blocks)])
        step *= 2
    return held


def on_device(source, cell_width):
    depth, rows, width_x = source.shape
    peers, blocks = lax.axis_size("pa"), lax.axis_size("gz")
    devices = peers * blocks
    width_y = rows * peers
    owned = width_x // devices
    group = LANES // depth
    parts = rows // group

    cosines = halves(cosine_rows(width_x)[:, : width_x // 2].reshape(-1, 2, width_x // 2).swapaxes(0, 1).reshape(width_x, -1))
    order = order_y(np.arange(width_y), peers, parts, group)
    sines = sine_tables(peers, parts, group)
    got = exchange(call_forward(source, *cosines, owned, group), devices)

    own_k = jnp.arange(owned, dtype=jnp.int32) * devices + lax.axis_index(ALL)
    eigen_x, eigen_y = eigen_first(own_k, width_x)[:, None], eigen_second(jnp.asarray(order), width_y)[None]
    solve = call_coefficients(all_widths(cell_width, blocks), eigen_x, eigen_y, depth)
    back = call_middle(
        got, *sines, *solve,
        peers=peers, blocks=blocks, depth=depth, parts=parts, group=group, owned=owned,
    )
    return call_backward(exchange(back, devices), *cosines, source.shape, owned, group)


def solution(mesh):
    return jax.shard_map(
        on_device,
        mesh=mesh,
        in_specs=(P("gz", "pa", None), P("gz")),
        out_specs=P("gz", "pa", None),
        check_vma=False,
    )
```

time: 106 us -> 101 us (0.953)
  Pallas kernels: 21.4 us -> 15.6 us
  waiting for transfers between devices: 23.1 us -> 24.6 us
    pallas_call x1, Pallas kernels: 8.74 us -> 5.34 us  [call_middle(): pl.pallas_call(functools.partial(middle, peers=peers, blocks=blocks, dept...]
    pallas_call x2, Pallas kernels: 8.58 us -> 6.95 us  [the longest x1 4.68 us: call_forward(): pl.pallas_call(functools.partial(forward_x, owned=owned, group=group), na...]
  transfers between devices with their start and end apart: 5 -> 5, of which waited for: 5 -> 5; matrix products, arithmetic and copies ran while one was open for 2% -> 1% of each run, Pallas kernels for 4% -> 3%
where the time goes in v3:
time: 101 us
  blocking collectives  40 us (40%)
  waiting for transfers between devices  24.6 us (24%)
  starting transfers between devices  19 us (19%)
  Pallas kernels  15.6 us (15%)
  other arithmetic  1.45 us (1%)
    all_to_all x1, blocking collectives, exchange(): lax.all_to_all(flat, ALL, split_axis=0, concat_axis=0, tiled=True)  40 us
    all_to_all x1, starting transfers between devices, exchange(): lax.all_to_all(flat, ALL, split_axis=0, concat_axis=0, tiled=True)  15.7 us
    all_to_all x1, waiting for transfers between devices, exchange(): lax.all_to_all(flat, ALL, split_axis=0, concat_axis=0, tiled=True)  15.6 us
    ppermute x4, waiting for transfers between devices, all_widths(): lax.ppermute(held, 'gz', [(i, i ^ step) for i in range(blocks)])  9 us
    pallas_call x1, Pallas kernels, call_middle(): pl.pallas_call(functools.partial(middle, peers=peers, blocks=blocks, dept...  5.34 us
    pallas_call x1, Pallas kernels, call_forward(): pl.pallas_call(functools.partial(forward_x, owned=owned, group=group), na...  4.68 us
    ppermute x4, starting transfers between devices, all_widths(): lax.ppermute(held, 'gz', [(i, i ^ step) for i in range(blocks)])  3.38 us
    pallas_call x1, Pallas kernels, call_coefficients(): pl.pallas_call(functools.partial(coefficients, depth=depth, tile=wide //...  3.32 us
  transfers between devices with their start and end apart: 5, of which 5 were waited for; matrix products, arithmetic and copies ran while one was open for 1% of the time, Pallas kernels for 3%

profile of v3, /device:TPU:1, one launch (start us, length us, event | category | flops | bytes accessed | tf_op | source)
XLA Modules:
  0.0 100.8 jit_solution(7502342010254833210)
XLA Ops:
  0.0 4.7 %forward_x.1 = f32[2304,128]{1,0:T(8,128)} custom-call(f32[8,48,768]{2,1,0:T(8,128)} %src_ref.1, bf16[768,384]{1,0:T(8,128)(2,1)} %constant.34.clone.ch_in.ch_ref, bf16[768,384]{1,0:T(8,128)(2,1)} %constant.35.clone.cl_in.cl_ref), custom_call_target="tpu_custom_call" | custom-call | tf_op jit(solution)/shard_map/forward_x/pallas_call | solution.py:396
  4.7 0.0 copy-start.4
  4.7 0.0 copy-start.2
  4.7 0.0 copy-start.3
  4.7 15.7 %all-to-all-start = ((f32[256,1,1152]{2,1,0:T(1,128)}), f32[256,1,1152]{2,1,0:T(1,128)S(1)}, u32[]{:S(2)}, u32[]{:S(2)}) async-start(f32[256,1,1152]{2,1,0:T(1,128)} %bitcast), calls=%async_computation | async-start | bytes 2359296 | tf_op jit(solution)/shard_map/all_to_all | solution.py:473
  20.4 0.1 broadcast_select_fusion
  20.5 2.2 %collective-permute-start = (f32[16,128]{1,0:T(8,128)S(1)}, f32[16,128]{1,0:T(8,128)S(1)}, u32[]{:S(2)}, u32[]{:S(2)}) collective-permute-start(f32[16,128]{1,0:T(8,128)S(1)} %broadcast_select_fusion), channel_id=1, source_target_pairs={{0,1},{1,0},{2,3},{3,2},{4,5},{5,4},{6,7},{7,6},{8,9},{9,8},{10,11... | collective-permute-start | bytes 24584 | tf_op jit(solution)/shard_map/ppermute | solution.py:482
  22.7 0.8 collective-permute-done
  23.5 0.1 fusion
  23.6 0.0 collective-permute-start.1
  23.6 2.8 %collective-permute-done.1 = f32[16,128]{1,0:T(8,128)S(1)} collective-permute-done((f32[16,128]{1,0:T(8,128)S(1)}, f32[16,128]{1,0:T(8,128)S(1)}, u32[]{:S(2)}, u32[]{:S(2)}) %collective-permute-start.1) | collective-permute-done | bytes 8224 | tf_op jit(solution)/shard_map/ppermute | solution.py:482
  26.4 0.1 fusion.1
  26.5 1.2 %collective-permute-start.2 = (f32[16,128]{1,0:T(8,128)S(1)}, f32[16,128]{1,0:T(8,128)S(1)}, u32[]{:S(2)}, u32[]{:S(2)}) collective-permute-start(f32[16,128]{1,0:T(8,128)S(1)} %fusion.1), channel_id=1, source_target_pairs={{0,4},{1,5},{2,6},{3,7},{4,0},{5,1},{6,2},{7,3},{8,12},{9,13},{10,... | collective-permute-start | bytes 24584 | tf_op jit(solution)/shard_map/ppermute | solution.py:482
  27.7 3.2 %collective-permute-done.2 = f32[16,128]{1,0:T(8,128)S(1)} collective-permute-done((f32[16,128]{1,0:T(8,128)S(1)}, f32[16,128]{1,0:T(8,128)S(1)}, u32[]{:S(2)}, u32[]{:S(2)}) %collective-permute-start.2) | collective-permute-done | bytes 8224 | tf_op jit(solution)/shard_map/ppermute | solution.py:482
  30.8 0.6 multiply_multiply_fusion.ek_ref
  31.5 2.2 %collective-permute-done.3 = f32[16,128]{1,0:T(8,128)S(1)} collective-permute-done((f32[16,128]{1,0:T(8,128)S(1)}, f32[16,128]{1,0:T(8,128)S(1)}, u32[]{:S(2)}, u32[]{:S(2)}) %collective-permute-start.3) | collective-permute-done | bytes 8224 | tf_op jit(solution)/shard_map/ppermute | solution.py:482
  33.7 0.6 add.39.wid_in_ref
  34.3 3.3 %coefficients.1 = (f32[2,384,768]{2,1,0:T(8,128)}, f32[2,128,128]{2,1,0:T(8,128)}, f32[6,384,128]{2,1,0:T(8,128)}) custom-call(f32[16,128]{1,0:T(8,128)} %add.39.wid_in_ref, f32[3,1]{1,0:T(4,128)} %multiply_multiply_fusion.ek_ref, f32[1,768]{1,0:T(1,128)} %constant.49.el_ref), custom_call_target="tpu_custom_call" | custom-call | tf_op jit(solution)/shard_map/coefficients/pallas_call | solution.py:433
  37.6 15.6 %all-to-all-done = f32[256,1,1152]{2,1,0:T(1,128)S(1)} async-done(((f32[256,1,1152]{2,1,0:T(1,128)}), f32[256,1,1152]{2,1,0:T(1,128)S(1)}, u32[]{:S(2)}, u32[]{:S(2)}) %all-to-all-start) | async-done | bytes 1179680 | tf_op jit(solution)/shard_map/all_to_all | solution.py:473
  53.2 5.3 %middle.1 = f32[2304,128]{1,0:T(8,128)S(1)} custom-call(f32[2304,128]{1,0:T(8,128)S(1)} %bitcast.5, bf16[768,768]{1,0:T(8,128)(2,1)S(1)} %copy-done.3, bf16[768,768]{1,0:T(8,128)(2,1)S(1)} %copy-done.2, f32[2,384,768]{2,1,0:T(8,128)} %get-tuple-element.8.cell_in, f32[2,128,128]{2,1,0:T(8,128)} %get-tuple-element.9.link_in, ...), custom_call_target="tpu_custom_call" | custom-call | tf_op jit(solution)/shard_map/middle/pallas_call | solution.py:449
  58.5 0.0 copy-start
  58.6 0.0 copy-start.1
  58.6 40.0 %all_to_all.10 = f32[256,1,1152]{2,1,0:T(1,128)S(1)} all-to-all(f32[256,1,1152]{2,1,0:T(1,128)S(1)} %bitcast.6), channel_id=1, replica_groups=mesh['pa'=16,'gz'=16] {'pa','gz'}, dimensions={0} | all-to-all | bytes 2359296 | tf_op jit(solution)/shard_map/all_to_all | solution.py:473
  98.5 2.3 %backward_x.1 = f32[8,48,768]{2,1,0:T(8,128)} custom-call(f32[2304,128]{1,0:T(8,128)S(1)} %bitcast.4, bf16[768,384]{1,0:T(8,128)(2,1)S(1)} %copy-done.1, bf16[768,384]{1,0:T(8,128)(2,1)S(1)} %copy-done), custom_call_target="tpu_custom_call" | custom-call | tf_op jit(solution)/shard_map/backward_x/pallas_call | solution.py:413
  (9 shorter events, 0.0 us)
Async XLA Ops:
  4.7 15.7 %copy-start.4 = (f32[8]{0:T(128)S(1)}, f32[8]{0:T(128)}, u32[]{:S(2)}) copy-start(f32[8]{0:T(128)} %param.8) | copy-start | bytes 100
  4.7 48.5 %copy-start.2 = (bf16[768,768]{1,0:T(8,128)(2,1)S(1)}, bf16[768,768]{1,0:T(8,128)(2,1)}, u32[]{:S(2)}) copy-start(bf16[768,768]{1,0:T(8,128)(2,1)} %constant.37.clone.sl_ref) | copy-start | bytes 3538948
  4.7 48.5 %copy-start.3 = (bf16[768,768]{1,0:T(8,128)(2,1)S(1)}, bf16[768,768]{1,0:T(8,128)(2,1)}, u32[]{:S(2)}) copy-start(bf16[768,768]{1,0:T(8,128)(2,1)} %constant.36.clone.sh_ref) | copy-start | bytes 3538948
  4.7 48.5 %all-to-all-start = ((f32[256,1,1152]{2,1,0:T(1,128)}), f32[256,1,1152]{2,1,0:T(1,128)S(1)}, u32[]{:S(2)}, u32[]{:S(2)}) async-start(f32[256,1,1152]{2,1,0:T(1,128)} %bitcast), calls=%async_computation | async-start | bytes 2359296 | tf_op jit(solution)/shard_map/all_to_all | solution.py:473
  20.5 3.0 %collective-permute-start = (f32[16,128]{1,0:T(8,128)S(1)}, f32[16,128]{1,0:T(8,128)S(1)}, u32[]{:S(2)}, u32[]{:S(2)}) collective-permute-start(f32[16,128]{1,0:T(8,128)S(1)} %broadcast_select_fusion), channel_id=1, source_target_pairs={{0,1},{1,0},{2,3},{3,2},{4,5},{5,4},{6,7},{7,6},{8,9},{9,8},{10,11... | collective-permute-start | bytes 24584 | tf_op jit(solution)/shard_map/ppermute | solution.py:482
  23.6 2.8 %collective-permute-start.1 = (f32[16,128]{1,0:T(8,128)S(1)}, f32[16,128]{1,0:T(8,128)S(1)}, u32[]{:S(2)}, u32[]{:S(2)}) collective-permute-start(f32[16,128]{1,0:T(8,128)S(1)} %fusion), channel_id=1, source_target_pairs={{0,2},{1,3},{2,0},{3,1},{4,6},{5,7},{6,4},{7,5},{8,10},{9,11},{10,... | collective-permute-start | bytes 24584 | tf_op jit(solution)/shard_map/ppermute | solution.py:482
  26.5 4.3 %collective-permute-start.2 = (f32[16,128]{1,0:T(8,128)S(1)}, f32[16,128]{1,0:T(8,128)S(1)}, u32[]{:S(2)}, u32[]{:S(2)}) collective-permute-start(f32[16,128]{1,0:T(8,128)S(1)} %fusion.1), channel_id=1, source_target_pairs={{0,4},{1,5},{2,6},{3,7},{4,0},{5,1},{6,2},{7,3},{8,12},{9,13},{10,... | collective-permute-start | bytes 24584 | tf_op jit(solution)/shard_map/ppermute | solution.py:482
  30.8 2.8 %collective-permute-start.3 = (f32[16,128]{1,0:T(8,128)S(1)}, f32[16,128]{1,0:T(8,128)S(1)}, u32[]{:S(2)}, u32[]{:S(2)}) collective-permute-start(f32[16,128]{1,0:T(8,128)S(1)} %add.38), channel_id=1, source_target_pairs={{0,8},{1,9},{2,10},{3,11},{4,12},{5,13},{6,14},{7,15},{8,0},{9,1},... | collective-permute-start | bytes 24584 | tf_op jit(solution)/shard_map/ppermute | solution.py:482
  58.5 40.0 %copy-start = (bf16[768,384]{1,0:T(8,128)(2,1)S(1)}, bf16[768,384]{1,0:T(8,128)(2,1)}, u32[]{:S(2)}) copy-start(bf16[768,384]{1,0:T(8,128)(2,1)} %constant.35.clone.cl_in.cl_ref) | copy-start | bytes 1769476
  58.6 40.0 %copy-start.1 = (bf16[768,384]{1,0:T(8,128)(2,1)S(1)}, bf16[768,384]{1,0:T(8,128)(2,1)}, u32[]{:S(2)}) copy-start(bf16[768,384]{1,0:T(8,128)(2,1)} %constant.34.clone.ch_in.ch_ref) | copy-start | bytes 1769476

commit v4 on v3

--- a/solution.py
+++ b/solution.py
@@ -30,20 +30,34 @@
     return weights[:, None] * np.cos(phases * (math.pi / (2 * width)))
 
 
-def sine_rows(width):
-    k = np.arange(1, width + 1)
-    phases = k[:, None] * k[None, :] % (2 * (width + 1))
-    return math.sqrt(2.0 / (width + 1)) * np.sin(phases * (math.pi / (width + 1)))
-
-
 def order_y(values, peers, parts, group):
     return values.reshape(peers, parts, group).transpose(1, 0, 2).reshape(-1)
 
 
-def sine_tables(peers, parts, group):
+def sine_parts(peers, parts, group):
     width = peers * parts * group
-    order = order_y(np.arange(width), peers, parts, group)
-    return halves(sine_rows(width)[order][:, order])
+    coarse = group * np.arange(peers * parts).reshape(peers, parts).T.reshape(-1)
+    fine = np.arange(1, group + 1)
+    cell = order_y(np.arange(1, width + 1), peers, parts, group)
+    scale = math.sqrt(2.0 / (width + 1))
+
+    def both(rows, scale):
+        angle = rows[:, None] * cell[None] % (2 * (width + 1)) * (math.pi / (width + 1))
+        return [jnp.asarray((scale * f(angle)).astype(np.float32)) for f in (np.sin, np.cos)]
+
+    return both(coarse, scale) + both(fine, 1.0)
+
+
+def sine_table(cs_ref, cc_ref, fs_ref, fc_ref, high_ref, low_ref):
+    group = fs_ref.shape[0]
+
+    def rows(i, _):
+        here = pl.ds(i, 1)
+        at = pl.ds(pl.multiple_of(i * group, group), group)
+        high_ref[at, :], low_ref[at, :] = split(cs_ref[here, :] * fc_ref[...] + cc_ref[here, :] * fs_ref[...])
+        return 0
+
+    lax.fori_loop(0, cs_ref.shape[0], rows, 0)
 
 
 def eigen_first(wavenumber, width):
@@ -98,7 +112,7 @@
     return copies
 
 
-def forward_x(src_ref, ch_in, cl_in, out_ref, acc_ref, ch_ref, cl_ref, sems, *, owned, group):
+def forward_x(src_ref, ch_in, cl_in, out_ref, acc_ref, msg_ref, ch_ref, cl_ref, sems, *, owned, group):
     copies = start_copies(((ch_in, ch_ref), (cl_in, cl_ref)), sems)
     depth, rows, width = src_ref.shape
     parts = rows // group
@@ -112,16 +126,22 @@
     folded = split(near + far), split(near - far)
     for copy in copies:
         copy.wait()
+    copies = []
     for odd in range(2):
         at = pl.ds(odd * half, half)
         acc_ref[at, :] = dot3((ch_ref[at, :], cl_ref[at, :]), folded[odd], ((1,), (1,)))
         for t in range(each // SUB):
             for kk in range(owned):
                 for m in range(parts):
-                    row = (odd + 2 * SUB * t) * stride + kk * parts + m
-                    out_ref[pl.ds(row, SUB, stride=2 * stride), :] = acc_ref[
+                    row = (odd * each + t * SUB) * stride + kk * parts + m
+                    msg_ref[pl.ds(row, SUB, stride=stride), :] = acc_ref[
                         pl.ds(odd * half + kk * each + t * SUB, SUB), pl.ds(m * LANES, LANES)
                     ]
+        at = pl.ds(odd * each * stride, each * stride)
+        copies.append(pltpu.make_async_copy(msg_ref.at[at], out_ref.at[at], sems.at[2 + odd]))
+        copies[-1].start()
+    for copy in copies:
+        copy.wait()
 
 
 def backward_x(msg_ref, ch_ref, cl_ref, out_ref, z_ref, y_ref, part_ref, sems, *, owned, group):
@@ -134,9 +154,9 @@
         for t in range(each // SUB):
             for kk in range(owned):
                 for m in range(parts):
-                    row = (odd + 2 * SUB * t) * stride + kk * parts + m
+                    row = (odd * each + t * SUB) * stride + kk * parts + m
                     z_ref[pl.ds(odd * half + kk * each + t * SUB, SUB), pl.ds(m * LANES, LANES)] = msg_ref[
-                        pl.ds(row, SUB, stride=2 * stride), :
+                        pl.ds(row, SUB, stride=stride), :
                     ]
     for odd in range(2):
         at = pl.ds(odd * half, half)
@@ -396,14 +416,15 @@
     return pl.pallas_call(
         functools.partial(forward_x, owned=owned, group=group),
         name="forward_x",
-        out_shape=pltpu.VMEM((width * depth * rows // LANES, LANES), jnp.float32),
+        out_shape=jax.ShapeDtypeStruct((width * depth * rows // LANES, LANES), jnp.float32),
         in_specs=[WHOLE, HBM, HBM],
-        out_specs=WHOLE,
+        out_specs=HBM,
         scratch_shapes=[
             pltpu.VMEM((width, depth * rows), jnp.float32),
+            pltpu.VMEM((width * depth * rows // LANES, LANES), jnp.float32),
             pltpu.VMEM(high.shape, jnp.bfloat16),
             pltpu.VMEM(low.shape, jnp.bfloat16),
-            pltpu.SemaphoreType.DMA((2,)),
+            pltpu.SemaphoreType.DMA((4,)),
         ],
     )(source, *in_hbm(high, low))
 
@@ -424,6 +445,17 @@
         ],
         compiler_params=pltpu.CompilerParams(vmem_limit_bytes=40 * 2**20),
     )(*on_chip(message, high, low))
+
+
+def sine_tables(peers, parts, group):
+    width = peers * parts * group
+    return pl.pallas_call(
+        sine_table,
+        name="sine_table",
+        out_shape=[pltpu.VMEM((width, width), jnp.bfloat16)] * 2,
+        in_specs=[WHOLE] * 4,
+        out_specs=[WHOLE] * 2,
+    )(*sine_parts(peers, parts, group))
 
 
 def call_coefficients(widths, eigen_x, eigen_y, depth):
@@ -498,7 +530,8 @@
     sines = sine_tables(peers, parts, group)
     got = exchange(call_forward(source, *cosines, owned, group), devices)
 
-    own_k = jnp.arange(owned, dtype=jnp.int32) * devices + lax.axis_index(ALL)
+    device, half = lax.axis_index(ALL), devices // 2
+    own_k = 2 * (jnp.arange(owned, dtype=jnp.int32) * half + device % half) + device // half
     eigen_x, eigen_y = eigen_first(own_k, width_x)[:, None], eigen_second(jnp.asarray(order), width_y)[None]
     solve = call_coefficients(all_widths(cell_width, blocks), eigen_x, eigen_y, depth)
     back = call_middle(

time: 101 us -> 101 us (level)
  waiting for transfers between devices: 24.6 us -> 22.6 us
  Pallas kernels: 15.6 us -> 17.4 us
    ppermute x4, waiting for transfers between devices: 9 us -> 7.05 us  [all_widths(): lax.ppermute(held, 'gz', [(i, i ^ step) for i in range(blocks)])]
    pallas_call x0 -> x1, Pallas kernels: none -> 1.94 us  [sine_tables(): pl.pallas_call(sine_table, name='sine_table', out_shape=[pltpu.VMEM((widt...]
  transfers between devices with their start and end apart: 5 -> 5, of which waited for: 5 -> 5; matrix products, arithmetic and copies ran while one was open for 1% -> 1% of each run, Pallas kernels for 3% -> 5%
where the time goes in v4:
time: 101 us
  blocking collectives  40 us (40%)
  waiting for transfers between devices  22.6 us (22%)
  starting transfers between devices  19 us (19%)
  Pallas kernels  17.4 us (17%)
  other arithmetic  1.45 us (1%)
    all_to_all x1, blocking collectives, exchange(): lax.all_to_all(flat, ALL, split_axis=0, concat_axis=0, tiled=True)  40 us
    all_to_all x1, starting transfers between devices, exchange(): lax.all_to_all(flat, ALL, split_axis=0, concat_axis=0, tiled=True)  15.7 us
    all_to_all x1, waiting for transfers between devices, exchange(): lax.all_to_all(flat, ALL, split_axis=0, concat_axis=0, tiled=True)  15.6 us
    ppermute x4, waiting for transfers between devices, all_widths(): lax.ppermute(held, 'gz', [(i, i ^ step) for i in range(blocks)])  7.05 us
    pallas_call x1, Pallas kernels, call_middle(): pl.pallas_call(functools.partial(middle, peers=peers, blocks=blocks, dept...  5.36 us
    pallas_call x1, Pallas kernels, call_forward(): pl.pallas_call(functools.partial(forward_x, owned=owned, group=group), na...  4.5 us
    ppermute x4, starting transfers between devices, all_widths(): lax.ppermute(held, 'gz', [(i, i ^ step) for i in range(blocks)])  3.38 us
    pallas_call x1, Pallas kernels, call_coefficients(): pl.pallas_call(functools.partial(coefficients, depth=depth, tile=wide //...  3.33 us
  transfers between devices with their start and end apart: 5, of which 5 were waited for; matrix products, arithmetic and copies ran while one was open for 1% of the time, Pallas kernels for 5%

profile of v4, /device:TPU:1, one launch (start us, length us, event | category | flops | bytes accessed | tf_op | source)
XLA Modules:
  0.0 100.6 jit_solution(1087698075148624654)
XLA Ops:
  0.0 4.5 %forward_x.1 = f32[2304,128]{1,0:T(8,128)} custom-call(f32[8,48,768]{2,1,0:T(8,128)} %src_ref.1, bf16[768,384]{1,0:T(8,128)(2,1)} %constant.64.clone.ch_in.ch_ref, bf16[768,384]{1,0:T(8,128)(2,1)} %constant.65.clone.cl_in.cl_ref), custom_call_target="tpu_custom_call" | custom-call | tf_op jit(solution)/shard_map/forward_x/pallas_call | solution.py:416
  4.5 0.0 copy-start.2
  4.5 15.7 %all-to-all-start = ((f32[256,1,1152]{2,1,0:T(1,128)}), f32[256,1,1152]{2,1,0:T(1,128)S(1)}, u32[]{:S(2)}, u32[]{:S(2)}) async-start(f32[256,1,1152]{2,1,0:T(1,128)} %bitcast.7), calls=%async_computation | async-start | bytes 2359296 | tf_op jit(solution)/shard_map/all_to_all | solution.py:505
  20.2 0.1 broadcast_select_fusion
  20.3 2.2 %collective-permute-start = (f32[16,128]{1,0:T(8,128)S(1)}, f32[16,128]{1,0:T(8,128)S(1)}, u32[]{:S(2)}, u32[]{:S(2)}) collective-permute-start(f32[16,128]{1,0:T(8,128)S(1)} %broadcast_select_fusion), channel_id=1, source_target_pairs={{0,1},{1,0},{2,3},{3,2},{4,5},{5,4},{6,7},{7,6},{8,9},{9,8},{10,11... | collective-permute-start | bytes 24584 | tf_op jit(solution)/shard_map/ppermute | solution.py:514
  22.5 0.8 collective-permute-done
  23.3 0.1 fusion
  23.4 0.0 collective-permute-start.1
  23.4 2.8 %collective-permute-done.1 = f32[16,128]{1,0:T(8,128)S(1)} collective-permute-done((f32[16,128]{1,0:T(8,128)S(1)}, f32[16,128]{1,0:T(8,128)S(1)}, u32[]{:S(2)}, u32[]{:S(2)}) %collective-permute-start.1) | collective-permute-done | bytes 8224 | tf_op jit(solution)/shard_map/ppermute | solution.py:514
  26.2 0.1 fusion.1
  26.3 1.2 %collective-permute-start.2 = (f32[16,128]{1,0:T(8,128)S(1)}, f32[16,128]{1,0:T(8,128)S(1)}, u32[]{:S(2)}, u32[]{:S(2)}) collective-permute-start(f32[16,128]{1,0:T(8,128)S(1)} %fusion.1), channel_id=1, source_target_pairs={{0,4},{1,5},{2,6},{3,7},{4,0},{5,1},{6,2},{7,3},{8,12},{9,13},{10,... | collective-permute-start | bytes 24584 | tf_op jit(solution)/shard_map/ppermute | solution.py:514
  27.5 3.2 %collective-permute-done.2 = f32[16,128]{1,0:T(8,128)S(1)} collective-permute-done((f32[16,128]{1,0:T(8,128)S(1)}, f32[16,128]{1,0:T(8,128)S(1)}, u32[]{:S(2)}, u32[]{:S(2)}) %collective-permute-start.2) | collective-permute-done | bytes 8224 | tf_op jit(solution)/shard_map/ppermute | solution.py:514
  30.6 0.0 collective-permute-start.3
  30.6 0.6 multiply_multiply_fusion.ek_ref
  31.3 1.9 %sine_table.1 = (bf16[768,768]{1,0:T(8,128)(2,1)S(1)}, bf16[768,768]{1,0:T(8,128)(2,1)S(1)}) custom-call(f32[48,768]{1,0:T(8,128)} %constant.66.clone.cs_ref, f32[48,768]{1,0:T(8,128)} %constant.67.clone.cc_ref, f32[16,768]{1,0:T(8,128)} %constant.68.clone.fs_ref, f32[16,768]{1,0:T(8,128)} %constant.69.clone.fc_ref), custom_call_target="tpu_custom_call" | custom-call | tf_op jit(solution)/shard_map/sine_table/pallas_call | solution.py:452
  33.2 0.3 collective-permute-done.3
  33.5 0.6 add.57.wid_in_ref
  34.1 3.3 %coefficients.1 = (f32[2,384,768]{2,1,0:T(8,128)}, f32[2,128,128]{2,1,0:T(8,128)}, f32[6,384,128]{2,1,0:T(8,128)}) custom-call(f32[16,128]{1,0:T(8,128)} %add.57.wid_in_ref, f32[3,1]{1,0:T(4,128)} %multiply_multiply_fusion.ek_ref, f32[1,768]{1,0:T(1,128)} %constant.81.el_ref), custom_call_target="tpu_custom_call" | custom-call | tf_op jit(solution)/shard_map/coefficients/pallas_call | solution.py:465
  37.4 15.6 %all-to-all-done = f32[256,1,1152]{2,1,0:T(1,128)S(1)} async-done(((f32[256,1,1152]{2,1,0:T(1,128)}), f32[256,1,1152]{2,1,0:T(1,128)S(1)}, u32[]{:S(2)}, u32[]{:S(2)}) %all-to-all-start) | async-done | bytes 1179680 | tf_op jit(solution)/shard_map/all_to_all | solution.py:505
  53.0 5.4 %middle.1 = f32[2304,128]{1,0:T(8,128)S(1)} custom-call(f32[2304,128]{1,0:T(8,128)S(1)} %bitcast.5, bf16[768,768]{1,0:T(8,128)(2,1)S(1)} %get-tuple-element.10.sh_ref, bf16[768,768]{1,0:T(8,128)(2,1)S(1)} %get-tuple-element.11.sl_ref, f32[2,384,768]{2,1,0:T(8,128)} %get-tuple-element.12.cell_in, f32[2,128,128]{2,1,0:T(8,128)} %get-tuple-element.13.link_in, ...), custom_call_target="tpu_custom_call" | custom-call | tf_op jit(solution)/shard_map/middle/pallas_call | solution.py:481
  58.3 0.0 copy-start
  58.4 0.0 copy-start.1
  58.4 40.0 %all_to_all.10 = f32[256,1,1152]{2,1,0:T(1,128)S(1)} all-to-all(f32[256,1,1152]{2,1,0:T(1,128)S(1)} %bitcast.6), channel_id=1, replica_groups=mesh['pa'=16,'gz'=16] {'pa','gz'}, dimensions={0} | all-to-all | bytes 2359296 | tf_op jit(solution)/shard_map/all_to_all | solution.py:505
  98.3 2.3 %backward_x.1 = f32[8,48,768]{2,1,0:T(8,128)} custom-call(f32[2304,128]{1,0:T(8,128)S(1)} %bitcast.4, bf16[768,384]{1,0:T(8,128)(2,1)S(1)} %copy-done.1, bf16[768,384]{1,0:T(8,128)(2,1)S(1)} %copy-done), custom_call_target="tpu_custom_call" | custom-call | tf_op jit(solution)/shard_map/backward_x/pallas_call | solution.py:434
  (6 shorter events, 0.0 us)
Async XLA Ops:
  4.5 15.7 %copy-start.2 = (f32[8]{0:T(128)S(1)}, f32[8]{0:T(128)}, u32[]{:S(2)}) copy-start(f32[8]{0:T(128)} %param.10) | copy-start | bytes 100
  4.5 48.5 %all-to-all-start = ((f32[256,1,1152]{2,1,0:T(1,128)}), f32[256,1,1152]{2,1,0:T(1,128)S(1)}, u32[]{:S(2)}, u32[]{:S(2)}) async-start(f32[256,1,1152]{2,1,0:T(1,128)} %bitcast.7), calls=%async_computation | async-start | bytes 2359296 | tf_op jit(solution)/shard_map/all_to_all | solution.py:505
  20.3 3.0 %collective-permute-start = (f32[16,128]{1,0:T(8,128)S(1)}, f32[16,128]{1,0:T(8,128)S(1)}, u32[]{:S(2)}, u32[]{:S(2)}) collective-permute-start(f32[16,128]{1,0:T(8,128)S(1)} %broadcast_select_fusion), channel_id=1, source_target_pairs={{0,1},{1,0},{2,3},{3,2},{4,5},{5,4},{6,7},{7,6},{8,9},{9,8},{10,11... | collective-permute-start | bytes 24584 | tf_op jit(solution)/shard_map/ppermute | solution.py:514
  23.4 2.8 %collective-permute-start.1 = (f32[16,128]{1,0:T(8,128)S(1)}, f32[16,128]{1,0:T(8,128)S(1)}, u32[]{:S(2)}, u32[]{:S(2)}) collective-permute-start(f32[16,128]{1,0:T(8,128)S(1)} %fusion), channel_id=1, source_target_pairs={{0,2},{1,3},{2,0},{3,1},{4,6},{5,7},{6,4},{7,5},{8,10},{9,11},{10,... | collective-permute-start | bytes 24584 | tf_op jit(solution)/shard_map/ppermute | solution.py:514
  26.3 4.3 %collective-permute-start.2 = (f32[16,128]{1,0:T(8,128)S(1)}, f32[16,128]{1,0:T(8,128)S(1)}, u32[]{:S(2)}, u32[]{:S(2)}) collective-permute-start(f32[16,128]{1,0:T(8,128)S(1)} %fusion.1), channel_id=1, source_target_pairs={{0,4},{1,5},{2,6},{3,7},{4,0},{5,1},{6,2},{7,3},{8,12},{9,13},{10,... | collective-permute-start | bytes 24584 | tf_op jit(solution)/shard_map/ppermute | solution.py:514
  30.6 2.8 %collective-permute-start.3 = (f32[16,128]{1,0:T(8,128)S(1)}, f32[16,128]{1,0:T(8,128)S(1)}, u32[]{:S(2)}, u32[]{:S(2)}) collective-permute-start(f32[16,128]{1,0:T(8,128)S(1)} %add.56), channel_id=1, source_target_pairs={{0,8},{1,9},{2,10},{3,11},{4,12},{5,13},{6,14},{7,15},{8,0},{9,1},... | collective-permute-start | bytes 24584 | tf_op jit(solution)/shard_map/ppermute | solution.py:514
  58.3 40.0 %copy-start = (bf16[768,384]{1,0:T(8,128)(2,1)S(1)}, bf16[768,384]{1,0:T(8,128)(2,1)}, u32[]{:S(2)}) copy-start(bf16[768,384]{1,0:T(8,128)(2,1)} %constant.65.clone.cl_in.cl_ref) | copy-start | bytes 1769476
  58.4 40.0 %copy-start.1 = (bf16[768,384]{1,0:T(8,128)(2,1)S(1)}, bf16[768,384]{1,0:T(8,128)(2,1)}, u32[]{:S(2)}) copy-start(bf16[768,384]{1,0:T(8,128)(2,1)} %constant.64.clone.ch_in.ch_ref) | copy-start | bytes 1769476

commit v5 on v4

--- a/solution.py
+++ b/solution.py
@@ -112,24 +112,31 @@
     return copies
 
 
-def forward_x(src_ref, ch_in, cl_in, out_ref, acc_ref, msg_ref, ch_ref, cl_ref, sems, *, owned, group):
-    copies = start_copies(((ch_in, ch_ref), (cl_in, cl_ref)), sems)
-    depth, rows, width = src_ref.shape
+def forward_x(
+    src_in, ch_in, cl_in, out_ref, src_ref, xh_ref, xl_ref, acc_ref, msg_ref, ch_ref, cl_ref, sems, *, owned, group
+):
+    depth, rows, width = src_in.shape
     parts = rows // group
+    pieces = [(slice(None), pl.ds(m * group, group), slice(None)) for m in range(parts)]
+    copies = start_copies(
+        [(src_in.at[piece], src_ref.at[piece]) for piece in pieces] + [(ch_in, ch_ref), (cl_in, cl_ref)], sems
+    )
     half = width // 2
     each = half // owned
     stride = owned * parts
-    x = jnp.concatenate(
-        [src_ref[z, pl.ds(m * group, group), :] for m in range(parts) for z in range(depth)], 0
-    )
-    near, far = x[:, :half], mirrored(x[:, half:])
-    folded = split(near + far), split(near - far)
-    for copy in copies:
+    for m in range(parts):
+        copies[m].wait()
+        x = jnp.concatenate([src_ref[z, pl.ds(m * group, group), :] for z in range(depth)], 0)
+        near, far = x[:, :half], mirrored(x[:, half:])
+        at = pl.ds(m * depth * group, depth * group)
+        for odd, folded in enumerate((near + far, near - far)):
+            xh_ref[odd, at, :], xl_ref[odd, at, :] = split(folded)
+    for copy in copies[parts:]:
         copy.wait()
     copies = []
     for odd in range(2):
         at = pl.ds(odd * half, half)
-        acc_ref[at, :] = dot3((ch_ref[at, :], cl_ref[at, :]), folded[odd], ((1,), (1,)))
+        acc_ref[at, :] = dot3((ch_ref[at, :], cl_ref[at, :]), (xh_ref[odd], xl_ref[odd]), ((1,), (1,)))
         for t in range(each // SUB):
             for kk in range(owned):
                 for m in range(parts):
@@ -138,7 +145,7 @@
                         pl.ds(odd * half + kk * each + t * SUB, SUB), pl.ds(m * LANES, LANES)
                     ]
         at = pl.ds(odd * each * stride, each * stride)
-        copies.append(pltpu.make_async_copy(msg_ref.at[at], out_ref.at[at], sems.at[2 + odd]))
+        copies.append(pltpu.make_async_copy(msg_ref.at[at], out_ref.at[at], sems.at[parts + 2 + odd]))
         copies[-1].start()
     for copy in copies:
         copy.wait()
@@ -417,16 +424,19 @@
         functools.partial(forward_x, owned=owned, group=group),
         name="forward_x",
         out_shape=jax.ShapeDtypeStruct((width * depth * rows // LANES, LANES), jnp.float32),
-        in_specs=[WHOLE, HBM, HBM],
+        in_specs=[HBM] * 3,
         out_specs=HBM,
         scratch_shapes=[
+            pltpu.VMEM(source.shape, jnp.float32),
+            pltpu.VMEM((2, depth * rows, width // 2), jnp.bfloat16),
+            pltpu.VMEM((2, depth * rows, width // 2), jnp.bfloat16),
             pltpu.VMEM((width, depth * rows), jnp.float32),
             pltpu.VMEM((width * depth * rows // LANES, LANES), jnp.float32),
             pltpu.VMEM(high.shape, jnp.bfloat16),
             pltpu.VMEM(low.shape, jnp.bfloat16),
-            pltpu.SemaphoreType.DMA((4,)),
+            pltpu.SemaphoreType.DMA((rows // group + 4,)),
         ],
-    )(source, *in_hbm(high, low))
+    )(*in_hbm(source, high, low))
 
 
 def call_backward(message, high, low, shape, owned, group):
@@ -480,7 +490,7 @@
     size = (owned * depth * blocks, wide)
     return pl.pallas_call(
         functools.partial(
-            middle, peers=peers, blocks=blocks, depth=depth, parts=parts, group=group, owned=owned, tile=wide // 2
+            middle, peers=peers, blocks=blocks, depth=depth, parts=parts, group=group, owned=owned, tile=wide // 3
         ),
         name="middle",
         out_shape=pltpu.VMEM(message.shape, jnp.float32),

time: 101 us -> 100 us (0.990)
  no operation moved by 1% of the time
where the time goes in v5:
time: 100 us; the launch traced here: 99.7 us
  blocking collectives  40 us (40%)
  waiting for transfers between devices  22.6 us (23%)
  starting transfers between devices  19 us (19%)
  Pallas kernels  16.5 us (16%)
  other arithmetic  1.45 us (1%)
    all_to_all x1, blocking collectives, exchange(): lax.all_to_all(flat, ALL, split_axis=0, concat_axis=0, tiled=True)  40 us
    all_to_all x1, starting transfers between devices, exchange(): lax.all_to_all(flat, ALL, split_axis=0, concat_axis=0, tiled=True)  15.7 us
    all_to_all x1, waiting for transfers between devices, exchange(): lax.all_to_all(flat, ALL, split_axis=0, concat_axis=0, tiled=True)  15.6 us
    ppermute x4, waiting for transfers between devices, all_widths(): lax.ppermute(held, 'gz', [(i, i ^ step) for i in range(blocks)])  7.05 us
    pallas_call x1, Pallas kernels, call_middle(): pl.pallas_call(functools.partial(middle, peers=peers, blocks=blocks, dept...  5.37 us
    pallas_call x1, Pallas kernels, call_forward(): pl.pallas_call(functools.partial(forward_x, owned=owned, group=group), na...  3.62 us
    ppermute x4, starting transfers between devices, all_widths(): lax.ppermute(held, 'gz', [(i, i ^ step) for i in range(blocks)])  3.38 us
    pallas_call x1, Pallas kernels, call_coefficients(): pl.pallas_call(functools.partial(coefficients, depth=depth, tile=wide //...  3.33 us
  transfers between devices with their start and end apart: 5, of which 5 were waited for; matrix products, arithmetic and copies ran while one was open for 1% of the time, Pallas kernels for 5%

profile of v5, /device:TPU:1, one launch (start us, length us, event | category | flops | bytes accessed | tf_op | source)
XLA Modules:
  0.0 99.7 jit_solution(12910441231571338375)
XLA Ops:
  0.0 3.6 %forward_x.1 = f32[2304,128]{1,0:T(8,128)} custom-call(f32[8,48,768]{2,1,0:T(8,128)} %src_in.1, bf16[768,384]{1,0:T(8,128)(2,1)} %constant.64.clone.ch_in.ch_ref, bf16[768,384]{1,0:T(8,128)(2,1)} %constant.65.clone.cl_in.cl_ref), custom_call_target="tpu_custom_call" | custom-call | tf_op jit(solution)/shard_map/forward_x/pallas_call | solution.py:423
  3.6 0.0 copy-start.2
  3.6 15.7 %all-to-all-start = ((f32[256,1,1152]{2,1,0:T(1,128)}), f32[256,1,1152]{2,1,0:T(1,128)S(1)}, u32[]{:S(2)}, u32[]{:S(2)}) async-start(f32[256,1,1152]{2,1,0:T(1,128)} %bitcast.7), calls=%async_computation | async-start | bytes 2359296 | tf_op jit(solution)/shard_map/all_to_all | solution.py:515
  19.3 0.1 broadcast_select_fusion
  19.4 2.2 %collective-permute-start = (f32[16,128]{1,0:T(8,128)S(1)}, f32[16,128]{1,0:T(8,128)S(1)}, u32[]{:S(2)}, u32[]{:S(2)}) collective-permute-start(f32[16,128]{1,0:T(8,128)S(1)} %broadcast_select_fusion), channel_id=1, source_target_pairs={{0,1},{1,0},{2,3},{3,2},{4,5},{5,4},{6,7},{7,6},{8,9},{9,8},{10,11... | collective-permute-start | bytes 24584 | tf_op jit(solution)/shard_map/ppermute | solution.py:524
  21.6 0.8 collective-permute-done
  22.4 0.1 fusion
  22.5 0.0 collective-permute-start.1
  22.5 2.8 %collective-permute-done.1 = f32[16,128]{1,0:T(8,128)S(1)} collective-permute-done((f32[16,128]{1,0:T(8,128)S(1)}, f32[16,128]{1,0:T(8,128)S(1)}, u32[]{:S(2)}, u32[]{:S(2)}) %collective-permute-start.1) | collective-permute-done | bytes 8224 | tf_op jit(solution)/shard_map/ppermute | solution.py:524
  25.3 0.1 fusion.1
  25.4 1.2 %collective-permute-start.2 = (f32[16,128]{1,0:T(8,128)S(1)}, f32[16,128]{1,0:T(8,128)S(1)}, u32[]{:S(2)}, u32[]{:S(2)}) collective-permute-start(f32[16,128]{1,0:T(8,128)S(1)} %fusion.1), channel_id=1, source_target_pairs={{0,4},{1,5},{2,6},{3,7},{4,0},{5,1},{6,2},{7,3},{8,12},{9,13},{10,... | collective-permute-start | bytes 24584 | tf_op jit(solution)/shard_map/ppermute | solution.py:524
  26.6 3.2 %collective-permute-done.2 = f32[16,128]{1,0:T(8,128)S(1)} collective-permute-done((f32[16,128]{1,0:T(8,128)S(1)}, f32[16,128]{1,0:T(8,128)S(1)}, u32[]{:S(2)}, u32[]{:S(2)}) %collective-permute-start.2) | collective-permute-done | bytes 8224 | tf_op jit(solution)/shard_map/ppermute | solution.py:524
  29.7 0.0 collective-permute-start.3
  29.7 0.6 multiply_multiply_fusion.ek_ref
  30.4 1.9 %sine_table.1 = (bf16[768,768]{1,0:T(8,128)(2,1)S(1)}, bf16[768,768]{1,0:T(8,128)(2,1)S(1)}) custom-call(f32[48,768]{1,0:T(8,128)} %constant.66.clone.cs_ref, f32[48,768]{1,0:T(8,128)} %constant.67.clone.cc_ref, f32[16,768]{1,0:T(8,128)} %constant.68.clone.fs_ref, f32[16,768]{1,0:T(8,128)} %constant.69.clone.fc_ref), custom_call_target="tpu_custom_call" | custom-call | tf_op jit(solution)/shard_map/sine_table/pallas_call | solution.py:462
  32.3 0.3 collective-permute-done.3
  32.6 0.6 add.57.wid_in_ref
  33.2 3.3 %coefficients.1 = (f32[2,384,768]{2,1,0:T(8,128)}, f32[2,128,128]{2,1,0:T(8,128)}, f32[6,384,128]{2,1,0:T(8,128)}) custom-call(f32[16,128]{1,0:T(8,128)} %add.57.wid_in_ref, f32[3,1]{1,0:T(4,128)} %multiply_multiply_fusion.ek_ref, f32[1,768]{1,0:T(1,128)} %constant.81.el_ref), custom_call_target="tpu_custom_call" | custom-call | tf_op jit(solution)/shard_map/coefficients/pallas_call | solution.py:475
  36.5 15.6 %all-to-all-done = f32[256,1,1152]{2,1,0:T(1,128)S(1)} async-done(((f32[256,1,1152]{2,1,0:T(1,128)}), f32[256,1,1152]{2,1,0:T(1,128)S(1)}, u32[]{:S(2)}, u32[]{:S(2)}) %all-to-all-start) | async-done | bytes 1179680 | tf_op jit(solution)/shard_map/all_to_all | solution.py:515
  52.1 5.4 %middle.1 = f32[2304,128]{1,0:T(8,128)S(1)} custom-call(f32[2304,128]{1,0:T(8,128)S(1)} %bitcast.5, bf16[768,768]{1,0:T(8,128)(2,1)S(1)} %get-tuple-element.10.sh_ref, bf16[768,768]{1,0:T(8,128)(2,1)S(1)} %get-tuple-element.11.sl_ref, f32[2,384,768]{2,1,0:T(8,128)} %get-tuple-element.12.cell_in, f32[2,128,128]{2,1,0:T(8,128)} %get-tuple-element.13.link_in, ...), custom_call_target="tpu_custom_call" | custom-call | tf_op jit(solution)/shard_map/middle/pallas_call | solution.py:491
  57.5 0.0 copy-start
  57.5 0.0 copy-start.1
  57.5 40.0 %all_to_all.10 = f32[256,1,1152]{2,1,0:T(1,128)S(1)} all-to-all(f32[256,1,1152]{2,1,0:T(1,128)S(1)} %bitcast.6), channel_id=1, replica_groups=mesh['pa'=16,'gz'=16] {'pa','gz'}, dimensions={0} | all-to-all | bytes 2359296 | tf_op jit(solution)/shard_map/all_to_all | solution.py:515
  97.5 2.3 %backward_x.1 = f32[8,48,768]{2,1,0:T(8,128)} custom-call(f32[2304,128]{1,0:T(8,128)S(1)} %bitcast.4, bf16[768,384]{1,0:T(8,128)(2,1)S(1)} %copy-done.1, bf16[768,384]{1,0:T(8,128)(2,1)S(1)} %copy-done), custom_call_target="tpu_custom_call" | custom-call | tf_op jit(solution)/shard_map/backward_x/pallas_call | solution.py:444
  (6 shorter events, 0.0 us)
Async XLA Ops:
  3.6 15.7 %copy-start.2 = (f32[8]{0:T(128)S(1)}, f32[8]{0:T(128)}, u32[]{:S(2)}) copy-start(f32[8]{0:T(128)} %param.10) | copy-start | bytes 100
  3.6 48.5 %all-to-all-start = ((f32[256,1,1152]{2,1,0:T(1,128)}), f32[256,1,1152]{2,1,0:T(1,128)S(1)}, u32[]{:S(2)}, u32[]{:S(2)}) async-start(f32[256,1,1152]{2,1,0:T(1,128)} %bitcast.7), calls=%async_computation | async-start | bytes 2359296 | tf_op jit(solution)/shard_map/all_to_all | solution.py:515
  19.4 3.0 %collective-permute-start = (f32[16,128]{1,0:T(8,128)S(1)}, f32[16,128]{1,0:T(8,128)S(1)}, u32[]{:S(2)}, u32[]{:S(2)}) collective-permute-start(f32[16,128]{1,0:T(8,128)S(1)} %broadcast_select_fusion), channel_id=1, source_target_pairs={{0,1},{1,0},{2,3},{3,2},{4,5},{5,4},{6,7},{7,6},{8,9},{9,8},{10,11... | collective-permute-start | bytes 24584 | tf_op jit(solution)/shard_map/ppermute | solution.py:524
  22.5 2.8 %collective-permute-start.1 = (f32[16,128]{1,0:T(8,128)S(1)}, f32[16,128]{1,0:T(8,128)S(1)}, u32[]{:S(2)}, u32[]{:S(2)}) collective-permute-start(f32[16,128]{1,0:T(8,128)S(1)} %fusion), channel_id=1, source_target_pairs={{0,2},{1,3},{2,0},{3,1},{4,6},{5,7},{6,4},{7,5},{8,10},{9,11},{10,... | collective-permute-start | bytes 24584 | tf_op jit(solution)/shard_map/ppermute | solution.py:524
  25.4 4.3 %collective-permute-start.2 = (f32[16,128]{1,0:T(8,128)S(1)}, f32[16,128]{1,0:T(8,128)S(1)}, u32[]{:S(2)}, u32[]{:S(2)}) collective-permute-start(f32[16,128]{1,0:T(8,128)S(1)} %fusion.1), channel_id=1, source_target_pairs={{0,4},{1,5},{2,6},{3,7},{4,0},{5,1},{6,2},{7,3},{8,12},{9,13},{10,... | collective-permute-start | bytes 24584 | tf_op jit(solution)/shard_map/ppermute | solution.py:524
  29.7 2.8 %collective-permute-start.3 = (f32[16,128]{1,0:T(8,128)S(1)}, f32[16,128]{1,0:T(8,128)S(1)}, u32[]{:S(2)}, u32[]{:S(2)}) collective-permute-start(f32[16,128]{1,0:T(8,128)S(1)} %add.56), channel_id=1, source_target_pairs={{0,8},{1,9},{2,10},{3,11},{4,12},{5,13},{6,14},{7,15},{8,0},{9,1},... | collective-permute-start | bytes 24584 | tf_op jit(solution)/shard_map/ppermute | solution.py:524
  57.5 40.0 %copy-start = (bf16[768,384]{1,0:T(8,128)(2,1)S(1)}, bf16[768,384]{1,0:T(8,128)(2,1)}, u32[]{:S(2)}) copy-start(bf16[768,384]{1,0:T(8,128)(2,1)} %constant.65.clone.cl_in.cl_ref) | copy-start | bytes 1769476
  57.5 40.0 %copy-start.1 = (bf16[768,384]{1,0:T(8,128)(2,1)S(1)}, bf16[768,384]{1,0:T(8,128)(2,1)}, u32[]{:S(2)}) copy-start(bf16[768,384]{1,0:T(8,128)(2,1)} %constant.64.clone.ch_in.ch_ref) | copy-start | bytes 1769476
